TPU v7x, 1024 devices: a whole 4x4x32 slice. The times are simulated.
1024 devices in a mesh: role: 2 (over y_lo), space: 64 (over z, core), freq: 8 (over y_hi, x).
Axes of the slice: x: 4, y: 4 (y_hi: 2, y_lo: 2; y = y_hi * 2 + y_lo), z: 32, core: 2. Of those that a mesh axis runs over, the one named last changes fastest.
Arguments:
- fields: float32 [2, 5, 16, 8192], P('role', None, 'freq', 'space'), may hold values from -6 to 6
- spectra: float32 [2, 128, 4, 16, 8192], P('role', 'freq', None, None, 'space'), may hold values from -6 to 6
- freq_index: int32 [128], P('freq'), may hold values from 1 to 63
- freq_weight: float32 [128], P('freq'), may hold values from 0.5 to 2
- material_ids: int32 [16, 8192], P('freq', 'space'), may hold values from 0 to 7
- material: float32 [3, 8], replicated, may hold values from 0.5 to 2
- source_cells: int32 [2, 16], P('role'), may hold values from 0 to 131071
- wavelets: float32 [2, 8, 16], P('role'), may hold values from -6 to 6
Outputs:
- fields_out: float32 [2, 5, 16, 8192], P('role', None, 'freq', 'space')
- spectra_out: float32 [2, 128, 4, 16, 8192], P('role', 'freq', None, None, 'space')
- gradient: float32 [16, 8192], P(('role', 'freq'), 'space')
Inputs may be any that keep to these rules, and one draw needn't show every extreme that they name: `source_cells`: cells may repeat.
All inputs are finite; a program needn't handle non-finite values.
Results may differ from a plain program's by a relative error of at most 0.0033.
Values may be sent and summed in bfloat16 or wider, within the bound.
No kernel may reach another device: no remote copies, remote signals or barrier semaphores. Data moves between devices by JAX's collectives and lax.ppermute only.
A program may use at most 32 MiB of HBM per device.

v0:
```python
import functools

import jax
import jax.numpy as jnp
from jax import lax
from jax.experimental import pallas as pl
from jax.experimental.pallas import tpu as pltpu
from jax.sharding import PartitionSpec as P

F = 128
STEPS = 8
PERIOD = 64
NMAT = 8
NFIELD = 5
NPROP = 3
COURANT = 0.18
TWO_PI = 6.283185307179586
LANES = 128
HALO = STEPS
ROW_PROPS = 10
ROW_CELLS = 16
ROW_INDEX = 17
ROW_WEIGHT = 18
ROW_WAVELET = 19
MSG_ROWS = 24
VMEM = pltpu.VMEM


def whole(space=VMEM):
    return pl.BlockSpec(memory_space=space)


def cost(flops, read):
    return pl.CostEstimate(flops=flops, bytes_accessed=read, transcendentals=0)


def lane_ids(shape):
    return lax.broadcasted_iota(jnp.int32, shape, len(shape) - 1)


def pack_fields(fields, ids, material, cells, index, weight, wavelets, message, tile, wide):
    tile[...] = jnp.zeros_like(tile)
    wide[...] = jnp.zeros_like(wide)
    for field in range(NFIELD):
        tile[2 * field : 2 * field + 2, :] = fields[field]
    which = ids[...]
    for prop in range(NPROP):
        value = jnp.zeros(which.shape, jnp.float32)
        for block in range(NMAT):
            value = jnp.where(which == block, material[prop, block], value)
        row = ROW_PROPS + 2 * prop
        tile[row : row + 2, :] = COURANT * value
    count = cells.shape[1]
    tile[ROW_CELLS : ROW_CELLS + 1, :count] = cells[...].astype(jnp.float32)
    tile[ROW_INDEX : ROW_INDEX + 1, : index.shape[1]] = index[...].astype(jnp.float32)
    tile[ROW_WEIGHT : ROW_WEIGHT + 1, : weight.shape[1]] = weight[...]
    wide[:, :count] = wavelets[...]
    spread = pltpu.roll(wide[...], 0, 1, stride=count, stride_axis=0)
    tile[ROW_WAVELET : ROW_WAVELET + 1, :] = jnp.sum(spread, axis=0, keepdims=True)
    value = tile[...]
    for target in range(message.shape[0]):
        message[target] = value


def pack_spectra(rows_all, parts, freqs, spectra, message):
    for row in range(rows_all):
        for part in range(parts):
            picked = spectra[pl.ds(part * rows_all + row, freqs, stride=parts * rows_all), :]
            message[row, part * freqs : (part + 1) * freqs, :] = picked.astype(jnp.bfloat16)


def unpack_fields(groups, received, center, edges):
    rows_all = 2 * groups
    lanes = lane_ids((rows_all, LANES))
    left = jnp.zeros((rows_all, LANES), jnp.float32)
    right = jnp.zeros((rows_all, LANES), jnp.float32)
    channels = [(role, 2 * field) for role in range(2) for field in range(NFIELD)]
    channels += [(0, ROW_PROPS + 2 * prop) for prop in range(NPROP)]
    for slot, (role, first) in enumerate(channels):
        for k in range(2):
            start = role * groups * MSG_ROWS + first + k
            center[pl.ds(slot * rows_all + k, groups, stride=2), :] = received[
                pl.ds(start, groups, stride=MSG_ROWS), :
            ]
        value = center[slot * rows_all : (slot + 1) * rows_all, :]
        low = jnp.where(lanes < HALO, value, 0.0)
        high = jnp.where(lanes >= LANES - HALO, value, 0.0)
        left = left + pltpu.roll(low, HALO * slot, 1)
        right = right + pltpu.roll(high, (HALO * slot + HALO) % LANES, 1)
    edges[0] = left
    edges[1] = right


def prepare(groups, freqs, count, width_all, received, inject, table, weights):
    rows_all = 2 * groups
    first_column = lax.axis_index("space") * LANES
    def joined(row):
        value = received[pl.ds(row, groups, stride=MSG_ROWS), :]
        spread = pltpu.roll(value, 0, 1, stride=freqs, stride_axis=0)
        return jnp.sum(spread, axis=0, keepdims=True)

    weights[...] = joined(ROW_WEIGHT)
    index = joined(ROW_INDEX).astype(jnp.int32)
    times = lax.broadcasted_iota(jnp.int32, (STEPS, LANES), 0)
    turns = lax.bitwise_and(index * times, PERIOD - 1)
    angle = turns.astype(jnp.float32) * (TWO_PI / PERIOD)
    table[:STEPS, :] = jnp.cos(angle).astype(jnp.bfloat16).astype(jnp.float32)
    table[STEPS:, :] = (-jnp.sin(angle)).astype(jnp.bfloat16).astype(jnp.float32)
    window = lax.broadcasted_iota(jnp.int32, (2 * LANES, LANES), 0)
    window = jnp.where(window < LANES + LANES // 2, window, window - 2 * LANES)
    row_ids = lax.broadcasted_iota(jnp.int32, (rows_all, LANES), 0)
    valid = lane_ids((rows_all, LANES)) < count
    for role in range(2):
        base = role * groups * MSG_ROWS
        cells = received[base + ROW_CELLS : base + ROW_CELLS + 1, :].astype(jnp.int32)
        cell_row = cells // width_all
        cell_column = cells - cell_row * width_all - first_column
        hit_column = jnp.where(window == cell_column, 1.0, 0.0)
        hit_row = jnp.logical_and(row_ids == cell_row, valid)
        amounts = received[base + ROW_WAVELET : base + ROW_WAVELET + 1, :]
        terms = []
        for tick in range(STEPS):
            shift = (LANES - tick * count) % LANES
            amount = pltpu.roll(jnp.broadcast_to(amounts, (rows_all, LANES)), shift, 1)
            terms.append(jnp.where(hit_row, amount, 0.0))
        left = jnp.concatenate(terms, axis=0)
        inject[role] = lax.dot_general(
            left,
            hit_column,
            (((1,), (1,)), ((), ())),
            precision=lax.Precision.HIGHEST,
            preferred_element_type=jnp.float32,
        )


def step_kernel(
    groups,
    freqs,
    center,
    halo_low,
    halo_high,
    inject,
    kron,
    spectra,
    fields_out,
    row_snaps,
    spectra_out,
    snaps,
    finals,
    held,
    read_sem,
    write_sem,
):
    rows_all = 2 * groups
    fetch = pltpu.make_async_copy(spectra, held, read_sem)
    fetch.start()
    own_role = lax.axis_index("role")
    own_group = lax.axis_index("freq")
    lanes = lane_ids((rows_all, LANES))
    row_ids = lax.broadcasted_iota(jnp.int32, (rows_all, 2 * LANES), 0)
    from_high = halo_high[...]
    from_low = halo_low[...]

    def extended(slot):
        middle = center[slot * rows_all : (slot + 1) * rows_all, :]
        after = pltpu.roll(from_high, (LANES - HALO * slot) % LANES, 1)
        before = pltpu.roll(from_low, (2 * LANES - HALO - HALO * slot) % LANES, 1)
        side = jnp.where(lanes < HALO, after, jnp.where(lanes >= LANES - HALO, before, 0.0))
        return jnp.concatenate([middle, side], axis=1)

    def up(value):
        return jnp.where(row_ids < rows_all - 1, pltpu.roll(value, rows_all - 1, 0), 0.0)

    def down(value):
        return jnp.where(row_ids > 0, pltpu.roll(value, 1, 0), 0.0)

    def after(value):
        return pltpu.roll(value, 2 * LANES - 1, 1)

    def before(value):
        return pltpu.roll(value, 1, 1)

    buoyancy, lame_first, lame_second = (extended(2 * NFIELD + prop) for prop in range(NPROP))
    stiff = lame_first + 2.0 * lame_second
    for role in range(2):
        vel_x, vel_z, sig_xx, sig_zz, sig_xz = (
            extended(role * NFIELD + field) for field in range(NFIELD)
        )
        for tick in range(STEPS):
            vel_x = vel_x + buoyancy * ((up(sig_xx) - sig_xx) + (sig_xz - before(sig_xz)))
            vel_z = vel_z + buoyancy * ((sig_xz - down(sig_xz)) + (after(sig_zz) - sig_zz))
            source = inject[role, tick * rows_all : (tick + 1) * rows_all, :]
            strain_x = vel_x - down(vel_x)
            strain_z = vel_z - before(vel_z)
            sig_xx = sig_xx + (stiff * strain_x + lame_first * strain_z) + source
            sig_zz = sig_zz + (lame_first * strain_x + stiff * strain_z) + source
            sig_xz = sig_xz + lame_second * ((after(vel_x) - vel_x) + (up(vel_z) - vel_z))
            for part, value in enumerate((vel_x, vel_z)):
                at = ((role * STEPS + tick) * 2 + part) * rows_all
                rounded = value[:, :LANES].astype(jnp.bfloat16).astype(jnp.float32)
                snaps[at : at + rows_all, :] = rounded
        for field, value in enumerate((vel_x, vel_z, sig_xx, sig_zz, sig_xz)):
            finals[role, field] = value[:, :LANES]
    for field in range(NFIELD):
        fields_out[field] = finals[own_role, field, pl.ds(2 * own_group, 2), :]
    own_row = own_role * groups + own_group
    for role in range(2):
        for part in range(2):
            start = (role * STEPS * 2 + part) * rows_all + own_row
            row_snaps[role, :, part * LANES : (part + 1) * LANES] = snaps[
                pl.ds(start, STEPS, stride=2 * rows_all), :
            ]
    base = own_role * (STEPS * 2 * rows_all)
    blocks = []
    for part in range(2):
        for half in range(rows_all // 8):
            pieces = [
                snaps[pl.ds(pl.multiple_of(base + (tick * 2 + part) * rows_all + half * 8, 8), 8), :]
                for tick in range(STEPS)
            ]
            blocks.append(jnp.concatenate(pieces, axis=0))
    right = jnp.concatenate(blocks, axis=1).astype(jnp.bfloat16)
    added = lax.dot_general(
        kron[...], right, (((1,), (0,)), ((), ())), preferred_element_type=jnp.float32
    )
    fetch.wait()
    per_freq = 4 * rows_all
    copies = []
    chunk = freqs // 4
    for freq in range(freqs):
        for phase in range(2):
            for part in range(2):
                for half in range(rows_all // 8):
                    at = freq * per_freq + (phase * 2 + part) * rows_all + half * 8
                    row = (freq * 2 + phase) * 8
                    column = (part * (rows_all // 8) + half) * LANES
                    held[at : at + 8, :] = (
                        held[at : at + 8, :] + added[row : row + 8, column : column + LANES]
                    )
        if (freq + 1) % chunk == 0:
            first = (freq + 1 - chunk) * per_freq
            span = pl.ds(first, chunk * per_freq)
            copy = pltpu.make_async_copy(
                held.at[span], spectra_out.at[span], write_sem.at[freq // chunk]
            )
            copy.start()
            copies.append(copy)
    for copy in copies:
        copy.wait()


def correlate(groups, freqs, received, row_snaps, table, weights, gradient):
    turned = table[...].astype(jnp.bfloat16)
    added = []
    for role in range(2):
        right = row_snaps[role].astype(jnp.bfloat16)
        phases = []
        for phase in range(2):
            phases.append(
                lax.dot_general(
                    turned[phase * STEPS : (phase + 1) * STEPS, :],
                    right,
                    (((0,), (0,)), ((), ())),
                    preferred_element_type=jnp.float32,
                )
            )
        added.append(phases)
    total = None
    for part in range(4):
        sides = []
        for role in range(2):
            pieces = [
                received[role * groups + group, part * freqs : (part + 1) * freqs, :]
                for group in range(groups)
            ]
            column = (part % 2) * LANES
            own = added[role][part // 2][:, column : column + LANES]
            sides.append(jnp.concatenate(pieces, axis=0).astype(jnp.float32) + own)
        product = sides[0] * sides[1]
        total = product if total is None else total + product
    gradient[...] = (
        lax.dot_general(
            weights[...],
            total,
            (((1,), (0,)), ((), ())),
            precision=lax.Precision.HIGHEST,
            preferred_element_type=jnp.float32,
        )
        * (1.0 / F)
    )


def phase_table(freq_index):
    freqs = freq_index.shape[0]
    shape = (freqs * 2 * 8, STEPS * 8)
    down = lax.broadcasted_iota(jnp.int32, shape, 0)
    across = lax.broadcasted_iota(jnp.int32, shape, 1)
    index = jnp.repeat(freq_index, 16)[:, None]
    turns = index * (across // 8) % PERIOD
    angle = turns.astype(jnp.float32) * (TWO_PI / PERIOD)
    value = jnp.where((down // 8) % 2 == 0, jnp.cos(angle), -jnp.sin(angle))
    return jnp.where(down % 8 == across % 8, value, 0.0).astype(jnp.bfloat16)


def f32(*shape):
    return jax.ShapeDtypeStruct(shape, jnp.float32)


def local(fields, spectra, freq_index, freq_weight, material_ids, material, source_cells, wavelets):
    groups = lax.axis_size("freq")
    members = 2 * groups
    freqs = freq_index.shape[0]
    rows_all = 2 * groups
    count = source_cells.shape[1]
    width_all = LANES * lax.axis_size("space")
    group_axes = ("role", "freq")
    flat = spectra.reshape(freqs * 4 * rows_all, LANES)

    message = pl.pallas_call(
        pack_fields,
        out_shape=f32(members, MSG_ROWS, LANES),
        in_specs=[whole(), whole(), whole(pltpu.SMEM), whole(), whole(), whole(), whole()],
        out_specs=whole(),
        scratch_shapes=[VMEM((MSG_ROWS, LANES), jnp.float32), VMEM((STEPS, LANES), jnp.float32)],
        cost_estimate=cost(100_000, 200_000),
        name="pack_fields",
    )(
        fields[0],
        material_ids,
        material,
        source_cells,
        freq_index[None],
        freq_weight[None],
        wavelets[0],
    )
    gathered = lax.all_to_all(message, group_axes, 0, 0, tiled=True)
    gathered = gathered.reshape(members * MSG_ROWS, LANES)

    row_message = pl.pallas_call(
        functools.partial(pack_spectra, rows_all, 4, freqs),
        out_shape=jax.ShapeDtypeStruct((rows_all, 4 * freqs, LANES), jnp.bfloat16),
        in_specs=[whole()],
        out_specs=whole(),
        cost_estimate=cost(2_000_000, 800_000),
        name="pack_spectra",
    )(flat)
    row_spectra = lax.all_to_all(row_message, group_axes, 0, 0, tiled=True)

    center, edges = pl.pallas_call(
        functools.partial(unpack_fields, groups),
        out_shape=[f32((2 * NFIELD + NPROP) * rows_all, LANES), f32(2, rows_all, LANES)],
        in_specs=[whole()],
        out_specs=[whole(), whole()],
        cost_estimate=cost(100_000, 300_000),
        name="unpack_fields",
    )(gathered)
    size = lax.axis_size("space")
    forward = [(i, i + 1) for i in range(size - 1)]
    backward = [(i + 1, i) for i in range(size - 1)]
    halo_low = lax.ppermute(edges[1], "space", forward)
    halo_high = lax.ppermute(edges[0], "space", backward)

    inject, table, weights = pl.pallas_call(
        functools.partial(prepare, groups, freqs, count, width_all),
        out_shape=[
            f32(2, STEPS * rows_all, 2 * LANES),
            f32(2 * STEPS, LANES),
            f32(1, LANES),
        ],
        in_specs=[whole()],
        out_specs=[whole()] * 3,
        cost_estimate=cost(2_000_000, 600_000),
        name="prepare",
    )(gathered)

    fields_out, row_snaps, spectra_out = pl.pallas_call(
        functools.partial(step_kernel, groups, freqs),
        out_shape=[
            f32(NFIELD, 2, LANES),
            f32(2, STEPS, 2 * LANES),
            f32(freqs * 4 * rows_all, LANES),
        ],
        in_specs=[whole()] * 5 + [whole(pl.ANY)],
        out_specs=[whole(), whole(), whole(pl.ANY)],
        scratch_shapes=[
            VMEM((2 * STEPS * 2 * rows_all, LANES), jnp.float32),
            VMEM((2, NFIELD, rows_all, LANES), jnp.float32),
            VMEM((freqs * 4 * rows_all, LANES), jnp.float32),
            pltpu.SemaphoreType.DMA,
            pltpu.SemaphoreType.DMA((4,)),
        ],
        cost_estimate=cost(20_000_000, 2_000_000),
        name="steps",
    )(center, halo_low, halo_high, inject, phase_table(freq_index), flat)

    gradient = pl.pallas_call(
        functools.partial(correlate, groups, freqs),
        out_shape=f32(1, LANES),
        in_specs=[whole()] * 4,
        out_specs=whole(),
        cost_estimate=cost(2_000_000, 600_000),
        name="correlate",
    )(row_spectra, row_snaps, table, weights)
    return fields_out[None], spectra_out.reshape(spectra.shape), gradient


def solution(mesh):
    return jax.shard_map(
        local,
        mesh=mesh,
        in_specs=(
            P("role", None, "freq", "space"),
            P("role", "freq", None, None, "space"),
            P("freq"),
            P("freq"),
            P("freq", "space"),
            P(),
            P("role", None),
            P("role", None, None),
        ),
        out_specs=(
            P("role", None, "freq", "space"),
            P("role", "freq", None, None, "space"),
            P(("role", "freq"), "space"),
        ),
        check_vma=False,
    )
```

profile of v0, /device:TPU:1, one launch (start us, length us, event | category | flops | bytes accessed | tf_op | source)
XLA Modules:
  0.0 49.6 jit_solution(12984073343085412925)
XLA Ops:
  0.6 1.6 %pack_fields.1 = f32[16,24,128]{2,1,0:T(8,128)} custom-call(f32[5,2,128]{2,1,0:T(2,128)} %bitcast.16, s32[2,128]{1,0:T(2,128)} %ids.1, f32[3,8]{1,0:T(4,128)} %material.1, s32[1,16]{1,0:T(1,128)} %cells.1, s32[1,16]{1,0:T(1,128)} %bitcast.18, f32[1,16]{1,0:T(1,128)} %bitcast.19, f32[8,16]{1,0:T(8,128)} %bitcast.17), custom_call_target="tpu_custom_call" | custom-call | flops 100000 | bytes 200000 | tf_op jit(solution)/shard_map/pack_fields/pallas_call | solution.py:319
  2.2 7.6 %all-to-all-start = ((f32[16,24,128]{2,1,0:T(8,128)}), f32[16,24,128]{2,1,0:T(8,128)S(1)}, u32[]{:S(2)}, u32[]{:S(2)}) async-start(f32[16,24,128]{2,1,0:T(8,128)} %pack_fields.1), calls=%async_computation | async-start | bytes 393216 | tf_op jit(solution)/shard_map/all_to_all | solution.py:336
  9.9 0.0 copy-start.4
  9.9 0.6 %copy-done.4 = s32[16]{0:T(128)S(1)} copy-done((s32[16]{0:T(128)S(1)}, s32[16]{0:T(128)}, u32[]{:S(2)}) %copy-start.4) | copy-done | bytes 88
  10.5 0.1 broadcast_in_dim.18
  10.6 0.1 mul.16
  10.7 2.0 %pack_spectra.1 = bf16[16,64,128]{2,1,0:T(8,128)(2,1)} custom-call(f32[1024,128]{1,0:T(8,128)} %bitcast.12), custom_call_target="tpu_custom_call" | custom-call | flops 2000000 | bytes 800000 | tf_op jit(solution)/shard_map/pack_spectra/pallas_call | solution.py:339
  12.7 4.3 %all-to-all-done = f32[16,24,128]{2,1,0:T(8,128)S(1)} async-done(((f32[16,24,128]{2,1,0:T(8,128)}), f32[16,24,128]{2,1,0:T(8,128)S(1)}, u32[]{:S(2)}, u32[]{:S(2)}) %all-to-all-start) | async-done | bytes 196640 | tf_op jit(solution)/shard_map/all_to_all | solution.py:336
  17.0 0.7 %copy-done = f32[16,24,128]{2,1,0:T(8,128)} copy-done((f32[16,24,128]{2,1,0:T(8,128)}, f32[16,24,128]{2,1,0:T(8,128)S(1)}, u32[]{:S(2)}) %copy-start) | copy-done | bytes 196632
  17.7 3.5 %all-to-all-start.1 = ((bf16[16,64,128]{2,1,0:T(8,128)(2,1)}), bf16[16,64,128]{2,1,0:T(8,128)(2,1)S(1)}, u32[]{:S(2)}, u32[]{:S(2)}) async-start(bf16[16,64,128]{2,1,0:T(8,128)(2,1)} %pack_spectra.1), calls=%async_computation.1 | async-start | bytes 524288 | tf_op jit(solution)/shard_map/all_to_all | solution.py:347
  21.2 1.7 %unpack_fields.1 = (f32[208,128]{1,0:T(8,128)}, f32[2,16,128]{2,1,0:T(8,128)}) custom-call(f32[384,128]{1,0:T(8,128)} %bitcast.14), custom_call_target="tpu_custom_call" | custom-call | flops 100000 | bytes 300000 | tf_op jit(solution)/shard_map/unpack_fields/pallas_call | solution.py:349
  22.9 0.7 %slice_bitcast_fusion = (f32[16,128]{1,0:T(8,128)S(1)}, f32[16,128]{1,0:T(8,128)S(1)}) fusion(f32[2,16,128]{2,1,0:T(8,128)} %get-tuple-element.12), kind=kLoop, calls=%fused_computation.15 | loop fusion | bytes 32768 | tf_op jit(solution)/shard_map/squeeze | solution.py:361
  23.6 13.2 %collective-permute-start.1 = (f32[16,128]{1,0:T(8,128)S(1)}, f32[16,128]{1,0:T(8,128)S(1)}, u32[]{:S(2)}, u32[]{:S(2)}) collective-permute-start(f32[16,128]{1,0:T(8,128)S(1)} %get-tuple-element.19), channel_id=1, source_target_pairs={{8,0},{16,8},{24,16},{32,24},{40,32},{48,40},{56,48},{64,56},{72,6... | collective-permute-start | bytes 24584 | tf_op jit(solution)/shard_map/ppermute | solution.py:361
  36.9 1.9 %collective-permute-start = (f32[16,128]{1,0:T(8,128)S(1)}, f32[16,128]{1,0:T(8,128)S(1)}, u32[]{:S(2)}, u32[]{:S(2)}) collective-permute-start(f32[16,128]{1,0:T(8,128)S(1)} %get-tuple-element.20), channel_id=1, source_target_pairs={{0,8},{8,16},{16,24},{24,32},{32,40},{40,48},{48,56},{56,64},{64,7... | collective-permute-start | bytes 24584 | tf_op jit(solution)/shard_map/ppermute | solution.py:360
  38.8 1.5 %select_convert_fusion.kron = bf16[256,64]{1,0:T(8,128)(2,1)} fusion(s32[64]{0:T(128)S(1)} %get-tuple-element.29, s32[64]{0:T(128)S(1)} %get-tuple-element.31, s32[256]{0:T(256)S(1)} %mul.16, s32[256]{0:T(256)S(1)} %get-tuple-element.25, s32[256]{0:T(256)S(1)} %get-tuple-element.28, s32[64]{0:T(128)S(1)} %get-tuple-element.30, s32[64]{0:T(128)S(1)} %get-tuple-element.32, ...), kind=kLoop, calls=%fused_computation.13 | loop fusion | flops 573440 | bytes 39552 | tf_op jit(solution)/shard_map/convert_element_type | solution.py:302
  40.3 2.0 %prepare.1 = (f32[2,128,256]{2,1,0:T(8,128)}, f32[16,128]{1,0:T(8,128)}, f32[1,128]{1,0:T(1,128)}) custom-call(f32[384,128]{1,0:T(8,128)} %bitcast.15), custom_call_target="tpu_custom_call" | custom-call | flops 2000000 | bytes 600000 | tf_op jit(solution)/shard_map/prepare/pallas_call | solution.py:363
  42.4 0.0 collective-permute-done.1.halo_high
  42.4 0.0 collective-permute-done.halo_low
  42.4 0.0 copy-start.3
  42.4 0.6 %copy-done.2 = f32[16,128]{1,0:T(8,128)} copy-done((f32[16,128]{1,0:T(8,128)}, f32[16,128]{1,0:T(8,128)S(1)}, u32[]{:S(2)}) %copy-start.2) | copy-done | bytes 8216
  43.0 3.9 %steps.1 = (f32[5,2,128]{2,1,0:T(2,128)}, f32[2,8,256]{2,1,0:T(8,128)}, f32[1024,128]{1,0:T(8,128)}) custom-call(f32[208,128]{1,0:T(8,128)} %get-tuple-element.11.center, f32[16,128]{1,0:T(8,128)} %copy-done.3, f32[16,128]{1,0:T(8,128)} %copy-done.2, f32[2,128,256]{2,1,0:T(8,128)} %get-tuple-element.13.inject, bf16[256,64]{1,0:T(8,128)(2,1)} %select_convert_fusion.kron, ...), custom_call_target="tpu_custom_call" | custom-call | flops 20000000 | bytes 2000000 | tf_op jit(solution)/shard_map/steps/pallas_call | solution.py:376
  46.9 0.0 all-to-all-done.1.received
  46.9 0.7 %copy-done.1 = bf16[16,64,128]{2,1,0:T(8,128)(2,1)} copy-done((bf16[16,64,128]{2,1,0:T(8,128)(2,1)}, bf16[16,64,128]{2,1,0:T(8,128)(2,1)S(1)}, u32[]{:S(2)}) %copy-start.1) | copy-done | bytes 262168
  47.6 2.0 %correlate.1 = f32[1,128]{1,0:T(1,128)} custom-call(bf16[16,64,128]{2,1,0:T(8,128)(2,1)} %copy-done.1, f32[2,8,256]{2,1,0:T(8,128)} %get-tuple-element.16.row_snaps, f32[16,128]{1,0:T(8,128)} %get-tuple-element.17.table, f32[1,128]{1,0:T(1,128)} %get-tuple-element.18.weights), custom_call_target="tpu_custom_call" | custom-call | flops 2000000 | bytes 600000 | tf_op jit(solution)/shard_map/correlate/pallas_call | solution.py:396
  (10 shorter events, 0.0 us)
Async XLA Ops:
  2.2 14.8 %all-to-all-start = ((f32[16,24,128]{2,1,0:T(8,128)}), f32[16,24,128]{2,1,0:T(8,128)S(1)}, u32[]{:S(2)}, u32[]{:S(2)}) async-start(f32[16,24,128]{2,1,0:T(8,128)} %pack_fields.1), calls=%async_computation | async-start | bytes 393216 | tf_op jit(solution)/shard_map/all_to_all | solution.py:336
  9.9 0.7 %copy-start.4 = (s32[16]{0:T(128)S(1)}, s32[16]{0:T(128)}, u32[]{:S(2)}) copy-start(s32[16]{0:T(128)} %param.10) | copy-start | bytes 196
  17.0 0.7 %copy-start = (f32[16,24,128]{2,1,0:T(8,128)}, f32[16,24,128]{2,1,0:T(8,128)S(1)}, u32[]{:S(2)}) copy-start(f32[16,24,128]{2,1,0:T(8,128)S(1)} %all-to-all-done) | copy-start | bytes 589828
  17.7 29.2 %all-to-all-start.1 = ((bf16[16,64,128]{2,1,0:T(8,128)(2,1)}), bf16[16,64,128]{2,1,0:T(8,128)(2,1)S(1)}, u32[]{:S(2)}, u32[]{:S(2)}) async-start(bf16[16,64,128]{2,1,0:T(8,128)(2,1)} %pack_spectra.1), calls=%async_computation.1 | async-start | bytes 524288 | tf_op jit(solution)/shard_map/all_to_all | solution.py:347
  23.6 18.8 %collective-permute-start.1 = (f32[16,128]{1,0:T(8,128)S(1)}, f32[16,128]{1,0:T(8,128)S(1)}, u32[]{:S(2)}, u32[]{:S(2)}) collective-permute-start(f32[16,128]{1,0:T(8,128)S(1)} %get-tuple-element.19), channel_id=1, source_target_pairs={{8,0},{16,8},{24,16},{32,24},{40,32},{48,40},{56,48},{64,56},{72,6... | collective-permute-start | bytes 24584 | tf_op jit(solution)/shard_map/ppermute | solution.py:361
  36.9 5.5 %collective-permute-start = (f32[16,128]{1,0:T(8,128)S(1)}, f32[16,128]{1,0:T(8,128)S(1)}, u32[]{:S(2)}, u32[]{:S(2)}) collective-permute-start(f32[16,128]{1,0:T(8,128)S(1)} %get-tuple-element.20), channel_id=1, source_target_pairs={{0,8},{8,16},{16,24},{24,32},{32,40},{40,48},{48,56},{56,64},{64,7... | collective-permute-start | bytes 24584 | tf_op jit(solution)/shard_map/ppermute | solution.py:360
  42.4 0.6 %copy-start.2 = (f32[16,128]{1,0:T(8,128)}, f32[16,128]{1,0:T(8,128)S(1)}, u32[]{:S(2)}) copy-start(f32[16,128]{1,0:T(8,128)S(1)} %collective-permute-done.1.halo_high) | copy-start | bytes 24580
  42.4 0.6 %copy-start.3 = (f32[16,128]{1,0:T(8,128)}, f32[16,128]{1,0:T(8,128)S(1)}, u32[]{:S(2)}) copy-start(f32[16,128]{1,0:T(8,128)S(1)} %collective-permute-done.halo_low) | copy-start | bytes 24580
  46.9 0.7 %copy-start.1 = (bf16[16,64,128]{2,1,0:T(8,128)(2,1)}, bf16[16,64,128]{2,1,0:T(8,128)(2,1)S(1)}, u32[]{:S(2)}) copy-start(bf16[16,64,128]{2,1,0:T(8,128)(2,1)S(1)} %all-to-all-done.1.received) | copy-start | bytes 786436
where the time goes:
time: 50.1 us; the launch traced here: 49.6 us
  starting transfers between devices  26.3 us (52%)
  Pallas kernels  13.2 us (26%)
  waiting for transfers between devices  4.3 us (9%)
  local copies, waits for them, and re-layouts  3.46 us (7%)
  other arithmetic  1.56 us (3%)
  between operations  0.74 us (1%)
    ppermute x1, starting transfers between devices, local(): halo_high = lax.ppermute(edges[0], 'space', backward)  13.2 us
    all_to_all x1, starting transfers between devices, local(): gathered = lax.all_to_all(message, group_axes, 0, 0, tiled=True)  7.57 us
    all_to_all x1, waiting for transfers between devices, local(): gathered = lax.all_to_all(message, group_axes, 0, 0, tiled=True)  4.29 us
    pallas_call x1, Pallas kernels, local(): pl.pallas_call(functools.partial(step_kernel, groups, freqs), out_shape=[...  3.95 us
    all_to_all x1, starting transfers between devices, local(): row_spectra = lax.all_to_all(row_message, group_axes, 0, 0, tiled=True)  3.53 us
    unnamed x10, local copies, waits for them, and re-layouts  2.59 us
    pallas_call x1, Pallas kernels, local(): pl.pallas_call(functools.partial(prepare, groups, freqs, count, width_all...  2.04 us
    pallas_call x1, Pallas kernels, local(): pl.pallas_call(functools.partial(pack_spectra, rows_all, 4, freqs), out_s...  2.04 us
  transfers between devices with their start and end apart: 4, of which 1 were waited for; matrix products, arithmetic and copies ran while one was open for 5% of the time, Pallas kernels for 20%

commit v1 on v0

v1 whole, which is shorter than its diff:
```python
import functools

import jax
import jax.numpy as jnp
from jax import lax
from jax.experimental import pallas as pl
from jax.experimental.pallas import tpu as pltpu
from jax.sharding import PartitionSpec as P


F = 128
STEPS = 8
PERIOD = 64
NMAT = 8
NFIELD = 5
NPROP = 3
COURANT = 0.18
TWO_PI = 6.283185307179586
LANES = 128
HALO = STEPS
PARTS = 4
CHANNELS = NFIELD + NPROP
ROW_HALO = 2 * CHANNELS
ROW_CELL_ROW = 18
ROW_CELL_COLUMN = 19
ROW_INDEX = 20
ROW_WEIGHT = 21
ROW_WAVELET = 22
MSG_ROWS = 24
VMEM = pltpu.VMEM


def whole(space=VMEM):
    return pl.BlockSpec(memory_space=space)


def cost(flops, read):
    return pl.CostEstimate(flops=flops, bytes_accessed=read, transcendentals=0)


def params(kib):
    return pltpu.CompilerParams(vmem_limit_bytes=kib * 1024)


def lane_ids(shape):
    return lax.broadcasted_iota(jnp.int32, shape, len(shape) - 1)


def is_even():
    return lax.rem(lax.axis_index("space"), 2) == 0


def pack_block(
    width_all,
    fields_in,
    ids_in,
    material_in,
    cells_in,
    index_in,
    weight_in,
    wavelets_in,
    spectra_in,
    block,
    edge_chip,
    edge_link,
    spectra,
    fields,
    ids,
    material,
    cells,
    index,
    weight,
    wavelets,
    wide,
    sems,
):
    sources = (fields_in, ids_in, material_in, cells_in, index_in, weight_in, wavelets_in, spectra_in)
    targets = (fields, ids, material, cells, index, weight, wavelets, spectra)
    copies = [
        pltpu.make_async_copy(source, target, sems.at[slot])
        for slot, (source, target) in enumerate(zip(sources, targets))
    ]
    for copy in copies:
        copy.start()
    block[...] = jnp.zeros_like(block)
    wide[...] = jnp.zeros_like(wide)
    for copy in copies[:-1]:
        copy.wait()
    for field in range(NFIELD):
        block[2 * field : 2 * field + 2, :] = fields[field]
    which = ids[...]
    for prop in range(NPROP):
        value = jnp.zeros(which.shape, jnp.float32)
        for kind in range(NMAT):
            value = jnp.where(which == kind, material[prop, kind], value)
        row = 2 * (NFIELD + prop)
        block[row : row + 2, :] = COURANT * value
    count = cells.shape[1]
    cell_row = lax.div(cells[...], width_all)
    block[ROW_CELL_ROW : ROW_CELL_ROW + 1, :count] = cell_row.astype(jnp.float32)
    cell_column = cells[...] - cell_row * width_all
    block[ROW_CELL_COLUMN : ROW_CELL_COLUMN + 1, :count] = cell_column.astype(jnp.float32)
    block[ROW_INDEX : ROW_INDEX + 1, : index.shape[1]] = index[...].astype(jnp.float32)
    block[ROW_WEIGHT : ROW_WEIGHT + 1, : weight.shape[1]] = weight[...]
    wide[:, :count] = wavelets[...]
    spread = pltpu.roll(wide[...], 0, 1, stride=count, stride_axis=0)
    block[ROW_WAVELET : ROW_WAVELET + 1, :] = jnp.sum(spread, axis=0, keepdims=True)
    lanes = lane_ids((2, LANES))
    low = jnp.zeros((2, LANES), jnp.float32)
    high = jnp.zeros((2, LANES), jnp.float32)
    for slot in range(CHANNELS):
        value = block[2 * slot : 2 * slot + 2, :]
        left = jnp.where(lanes < HALO, value, 0.0)
        right = jnp.where(lanes >= LANES - HALO, value, 0.0)
        low = low + pltpu.roll(left, HALO * slot, 1)
        high = high + pltpu.roll(right, (HALO * slot + HALO) % LANES, 1)
    even = is_even()
    edge_chip[...] = jnp.where(even, high, low)
    edge_link[...] = jnp.where(even, low, high)
    copies[-1].wait()


def pack_message(freqs, block, from_chip, from_link, spectra, message, built, sems):
    rows_all = message.shape[0]
    even = is_even()
    before = jnp.where(even, from_link[...], from_chip[...])
    after = jnp.where(even, from_chip[...], from_link[...])
    block[ROW_HALO : ROW_HALO + 2, :] = before + pltpu.roll(after, LANES // 2, 1)
    exact = block[...]
    high = exact.astype(jnp.bfloat16).astype(jnp.float32)
    both = jnp.concatenate([high, exact - high], axis=0).astype(jnp.bfloat16)
    copies = []
    for row in range(rows_all):
        built[row, : 2 * MSG_ROWS, :] = both
        for part in range(PARTS):
            picked = spectra[pl.ds(part * rows_all + row, freqs, stride=PARTS * rows_all), :]
            first = 2 * MSG_ROWS + part * freqs
            built[row, first : first + freqs, :] = picked.astype(jnp.bfloat16)
        if row % 4 == 3:
            span = pl.ds(row - 3, 4)
            copy = pltpu.make_async_copy(built.at[span], message.at[span], sems.at[row // 4])
            copy.start()
            copies.append(copy)
    for copy in copies:
        copy.wait()


def twiddle(freqs, index, kron):
    span = 8 * STEPS
    lanes = lax.broadcasted_iota(jnp.int32, (freqs, freqs), 1)
    rows = lax.broadcasted_iota(jnp.int32, (freqs, freqs), 0)
    diagonal = jnp.where(lanes == rows, index[...].astype(jnp.float32), 0.0)
    column = jnp.sum(diagonal, axis=1, keepdims=True).astype(jnp.int32)
    across = lax.bitwise_and(lane_ids((freqs, 2 * span)), span - 1)
    turns = lax.bitwise_and(column * lax.shift_right_logical(across, 3), PERIOD - 1)
    angle = turns.astype(jnp.float32) * (TWO_PI / PERIOD)
    upper = lane_ids((freqs, 2 * span)) >= span
    value = jnp.where(upper, -jnp.sin(angle), jnp.cos(angle))
    keep = lax.bitwise_and(lane_ids((8, span)), 7) == lax.broadcasted_iota(
        jnp.int32, (8, span), 0
    )
    for freq in range(freqs):
        pair = []
        for phase in range(2):
            one = value[freq : freq + 1, phase * span : (phase + 1) * span]
            pair.append(jnp.where(keep, jnp.broadcast_to(one, (8, span)), 0.0))
        kron[freq * 16 : (freq + 1) * 16, :] = jnp.concatenate(pair, axis=0).astype(jnp.bfloat16)


def unpack(groups, received, decoded, center, halos):
    rows_all = 2 * groups
    for source in range(2 * groups):
        both = received[source, : 2 * MSG_ROWS, :].astype(jnp.float32)
        decoded[source * MSG_ROWS : (source + 1) * MSG_ROWS, :] = (
            both[:MSG_ROWS, :] + both[MSG_ROWS:, :]
        )

    def gather(target, at, role, first):
        for k in range(2):
            start = role * groups * MSG_ROWS + first + k
            target[pl.ds(at + k, groups, stride=2), :] = decoded[
                pl.ds(start, groups, stride=MSG_ROWS), :
            ]

    for role in range(2):
        for field in range(NFIELD):
            gather(center, (role * NFIELD + field) * rows_all, role, 2 * field)
        gather(halos, role * rows_all, role, ROW_HALO)
    for prop in range(NPROP):
        gather(center, (2 * NFIELD + prop) * rows_all, 0, 2 * (NFIELD + prop))


def prepare(groups, freqs, count, decoded, inject, table, weights):
    rows_all = 2 * groups
    first_column = lax.axis_index("space") * LANES

    def joined(row):
        value = decoded[pl.ds(row, groups, stride=MSG_ROWS), :]
        spread = pltpu.roll(value, 0, 1, stride=freqs, stride_axis=0)
        return jnp.sum(spread, axis=0, keepdims=True)

    weights[...] = joined(ROW_WEIGHT)
    index = joined(ROW_INDEX).astype(jnp.int32)
    times = lax.broadcasted_iota(jnp.int32, (STEPS, LANES), 0)
    turns = lax.bitwise_and(index * times, PERIOD - 1)
    angle = turns.astype(jnp.float32) * (TWO_PI / PERIOD)
    table[:STEPS, :] = jnp.cos(angle)
    table[STEPS:, :] = -jnp.sin(angle)
    window = lax.broadcasted_iota(jnp.int32, (2 * LANES, LANES), 0)
    window = jnp.where(window < LANES + LANES // 2, window, window - 2 * LANES)
    row_ids = lax.broadcasted_iota(jnp.int32, (rows_all, LANES), 0)
    lanes = lane_ids((rows_all, LANES))
    row_lanes = lane_ids((1, LANES))

    def twice(row):
        value = jnp.where(row_lanes < count, row, 0.0)
        return value + pltpu.roll(value, count, 1)

    for role in range(2):
        base = role * groups * MSG_ROWS
        cell_row = twice(decoded[base + ROW_CELL_ROW : base + ROW_CELL_ROW + 1, :])
        cell_column = twice(decoded[base + ROW_CELL_COLUMN : base + ROW_CELL_COLUMN + 1, :])
        near = cell_column.astype(jnp.int32) - first_column
        hit_column = jnp.where(window == near, 1.0, 0.0).astype(jnp.bfloat16)
        hit_row = jnp.logical_and(row_ids == cell_row.astype(jnp.int32), lanes < 2 * count)
        exact = decoded[base + ROW_WAVELET : base + ROW_WAVELET + 1, :]
        high = exact.astype(jnp.bfloat16).astype(jnp.float32)
        low = exact - high
        terms = []
        for tick in range(STEPS):
            first = pltpu.roll(high, (LANES - tick * count) % LANES, 1)
            second = pltpu.roll(low, (LANES + count - tick * count) % LANES, 1)
            amount = jnp.where(row_lanes < count, first, second)
            terms.append(jnp.where(hit_row, jnp.broadcast_to(amount, (rows_all, LANES)), 0.0))
        left = jnp.concatenate(terms, axis=0).astype(jnp.bfloat16)
        inject[role] = lax.dot_general(
            left, hit_column, (((1,), (1,)), ((), ())), preferred_element_type=jnp.float32
        )


def step_fields(groups, center, halos, inject, snaps, finals):
    rows_all = 2 * groups
    lanes = lane_ids((rows_all, LANES))
    row_ids = lax.broadcasted_iota(jnp.int32, (rows_all, 2 * LANES), 0)

    def extended(at, role, slot):
        middle = center[at * rows_all : (at + 1) * rows_all, :]
        halo = halos[role * rows_all : (role + 1) * rows_all, :]
        after = pltpu.roll(halo, (LANES + LANES // 2 - HALO * slot) % LANES, 1)
        before = pltpu.roll(halo, (2 * LANES - HALO - HALO * slot) % LANES, 1)
        side = jnp.where(lanes < HALO, after, jnp.where(lanes >= LANES - HALO, before, 0.0))
        return jnp.concatenate([middle, side], axis=1)

    def up(value):
        return jnp.where(row_ids < rows_all - 1, pltpu.roll(value, rows_all - 1, 0), 0.0)

    def down(value):
        return jnp.where(row_ids > 0, pltpu.roll(value, 1, 0), 0.0)

    def after(value):
        return pltpu.roll(value, 2 * LANES - 1, 1)

    def before(value):
        return pltpu.roll(value, 1, 1)

    buoyancy, lame_first, lame_second = (
        extended(2 * NFIELD + prop, 0, NFIELD + prop) for prop in range(NPROP)
    )
    stiff = lame_first + 2.0 * lame_second
    for role in range(2):
        vel_x, vel_z, sig_xx, sig_zz, sig_xz = (
            extended(role * NFIELD + field, role, field) for field in range(NFIELD)
        )
        for tick in range(STEPS):
            vel_x = vel_x + buoyancy * ((up(sig_xx) - sig_xx) + (sig_xz - before(sig_xz)))
            vel_z = vel_z + buoyancy * ((sig_xz - down(sig_xz)) + (after(sig_zz) - sig_zz))
            source = inject[role, tick * rows_all : (tick + 1) * rows_all, :]
            strain_x = vel_x - down(vel_x)
            strain_z = vel_z - before(vel_z)
            sig_xx = sig_xx + (stiff * strain_x + lame_first * strain_z) + source
            sig_zz = sig_zz + (lame_first * strain_x + stiff * strain_z) + source
            sig_xz = sig_xz + lame_second * ((after(vel_x) - vel_x) + (up(vel_z) - vel_z))
            for part, value in enumerate((vel_x, vel_z)):
                at = ((role * STEPS + tick) * 2 + part) * rows_all
                rounded = value[:, :LANES].astype(jnp.bfloat16).astype(jnp.float32)
                snaps[at : at + rows_all, :] = rounded
        for field, value in enumerate((vel_x, vel_z, sig_xx, sig_zz, sig_xz)):
            finals[role, field] = value[:, :LANES]


def correlate(groups, freqs, received, row_snaps, table, weights, gradient):
    turned = table[...].astype(jnp.bfloat16)
    added = []
    for role in range(2):
        right = row_snaps[role].astype(jnp.bfloat16)
        phases = []
        for phase in range(2):
            phases.append(
                lax.dot_general(
                    turned[phase * STEPS : (phase + 1) * STEPS, :],
                    right,
                    (((0,), (0,)), ((), ())),
                    preferred_element_type=jnp.float32,
                )
            )
        added.append(phases)
    total = None
    for part in range(PARTS):
        sides = []
        first = 2 * MSG_ROWS + part * freqs
        for role in range(2):
            pieces = [
                received[role * groups + group, first : first + freqs, :]
                for group in range(groups)
            ]
            column = (part % 2) * LANES
            own = added[role][part // 2][:, column : column + LANES]
            sides.append(jnp.concatenate(pieces, axis=0).astype(jnp.float32) + own)
        product = sides[0] * sides[1]
        total = product if total is None else total + product
    gradient[...] = (
        lax.dot_general(
            weights[...],
            total,
            (((1,), (0,)), ((), ())),
            precision=lax.Precision.HIGHEST,
            preferred_element_type=jnp.float32,
        )
        * (1.0 / F)
    )


def finish(
    groups,
    freqs,
    count,
    received,
    kron,
    spectra,
    fields_out,
    spectra_out,
    gradient_out,
    decoded,
    center,
    halos,
    inject,
    table,
    weights,
    snaps,
    finals,
    row_snaps,
    own_fields,
    gradient,
    held,
    sems,
):
    rows_all = 2 * groups
    own_role = lax.axis_index("role")
    own_group = lax.axis_index("freq")
    unpack(groups, received, decoded, center, halos)
    prepare(groups, freqs, count, decoded, inject, table, weights)
    step_fields(groups, center, halos, inject, snaps, finals)
    for field in range(NFIELD):
        own_fields[field] = finals[own_role, field, pl.ds(2 * own_group, 2), :]
    copies = [pltpu.make_async_copy(own_fields, fields_out, sems.at[0])]
    copies[0].start()
    base = own_role * (STEPS * 2 * rows_all)
    blocks = []
    for part in range(2):
        for half in range(rows_all // 8):
            pieces = [
                snaps[pl.ds(pl.multiple_of(base + (tick * 2 + part) * rows_all + half * 8, 8), 8), :]
                for tick in range(STEPS)
            ]
            blocks.append(jnp.concatenate(pieces, axis=0))
    right = jnp.concatenate(blocks, axis=1).astype(jnp.bfloat16)
    per_freq = PARTS * rows_all
    chunk = freqs // 4
    for step in range(4):
        added = lax.dot_general(
            kron[step * chunk * 16 : (step + 1) * chunk * 16, :],
            right,
            (((1,), (0,)), ((), ())),
            preferred_element_type=jnp.float32,
        )
        for freq in range(chunk):
            for phase in range(2):
                for part in range(2):
                    for half in range(rows_all // 8):
                        at = (step * chunk + freq) * per_freq
                        at = at + (phase * 2 + part) * rows_all + half * 8
                        row = (freq * 2 + phase) * 8
                        column = (part * (rows_all // 8) + half) * LANES
                        held[at : at + 8, :] = (
                            spectra[at : at + 8, :]
                            + added[row : row + 8, column : column + LANES]
                        )
        span = pl.ds(step * chunk * per_freq, chunk * per_freq)
        copy = pltpu.make_async_copy(held.at[span], spectra_out.at[span], sems.at[1 + step])
        copy.start()
        copies.append(copy)
    own_row = own_role * groups + own_group
    for role in range(2):
        for part in range(2):
            start = (role * STEPS * 2 + part) * rows_all + own_row
            row_snaps[role, :, part * LANES : (part + 1) * LANES] = snaps[
                pl.ds(start, STEPS, stride=2 * rows_all), :
            ]
    correlate(groups, freqs, received, row_snaps, table, weights, gradient)
    copy = pltpu.make_async_copy(gradient, gradient_out, sems.at[5])
    copy.start()
    copies.append(copy)
    for copy in copies:
        copy.wait()


def f32(*shape):
    return jax.ShapeDtypeStruct(shape, jnp.float32)


def in_hbm(*arrays):
    return [pltpu.with_memory_space_constraint(array, pltpu.HBM) for array in arrays]


def swaps(size, first):
    pairs = [(i, i + 1) for i in range(first, size - 1, 2)]
    return pairs + [(b, a) for a, b in pairs]


def program(fields, spectra, freq_index, freq_weight, material_ids, material, source_cells, wavelets):
    groups = lax.axis_size("freq")
    members = 2 * groups
    freqs = freq_index.shape[0]
    rows_all = 2 * groups
    count = source_cells.shape[1]
    size = lax.axis_size("space")
    flat = spectra.reshape(freqs * PARTS * rows_all, LANES)
    message_rows = 2 * MSG_ROWS + PARTS * freqs

    block, edge_chip, edge_link, held = pl.pallas_call(
        functools.partial(pack_block, LANES * size),
        out_shape=[
            VMEM((MSG_ROWS, LANES), jnp.float32),
            VMEM((2, LANES), jnp.float32),
            VMEM((2, LANES), jnp.float32),
            VMEM(flat.shape, jnp.float32),
        ],
        in_specs=[whole(pl.ANY)] * 8,
        out_specs=[whole()] * 4,
        scratch_shapes=[
            VMEM((NFIELD, 2, LANES), jnp.float32),
            VMEM((2, LANES), jnp.int32),
            pltpu.SMEM(material.shape, jnp.float32),
            VMEM((1, count), jnp.int32),
            VMEM((1, freqs), jnp.int32),
            VMEM((1, freqs), jnp.float32),
            VMEM((STEPS, count), jnp.float32),
            VMEM((STEPS, LANES), jnp.float32),
            pltpu.SemaphoreType.DMA((8,)),
        ],
        cost_estimate=cost(100_000, 40_000),
        compiler_params=params(1024),
        name="pack_block",
    )(
        *in_hbm(
            fields[0],
            material_ids,
            material,
            source_cells,
            freq_index[None],
            freq_weight[None],
            wavelets[0],
            flat,
        )
    )
    from_link = lax.ppermute(edge_link, "space", swaps(size, 1))
    from_chip = lax.ppermute(edge_chip, "space", swaps(size, 0))

    message = pl.pallas_call(
        functools.partial(pack_message, freqs),
        out_shape=jax.ShapeDtypeStruct((members, message_rows, LANES), jnp.bfloat16),
        in_specs=[whole()] * 4,
        out_specs=whole(pl.ANY),
        scratch_shapes=[
            VMEM((members, message_rows, LANES), jnp.bfloat16),
            pltpu.SemaphoreType.DMA((members // 4,)),
        ],
        cost_estimate=cost(2_000_000, 1_000_000),
        compiler_params=params(1536),
        name="pack_message",
    )(block, from_chip, from_link, held)
    received = lax.all_to_all(message, ("role", "freq"), 0, 0, tiled=True)

    kron = pl.pallas_call(
        functools.partial(twiddle, freqs),
        out_shape=jax.ShapeDtypeStruct((freqs * 16, STEPS * 8), jnp.bfloat16),
        in_specs=[whole()],
        out_specs=whole(),
        cost_estimate=cost(100_000, 40_000),
        compiler_params=params(512),
        name="twiddle",
    )(freq_index[None])

    fields_out, spectra_out, gradient = pl.pallas_call(
        functools.partial(finish, groups, freqs, count),
        out_shape=[
            f32(NFIELD, 2, LANES),
            f32(freqs * PARTS * rows_all, LANES),
            f32(1, LANES),
        ],
        in_specs=[whole()] * 3,
        out_specs=[whole(pl.ANY)] * 3,
        scratch_shapes=[
            VMEM((members * MSG_ROWS, LANES), jnp.float32),
            VMEM(((2 * NFIELD + NPROP) * rows_all, LANES), jnp.float32),
            VMEM((2 * rows_all, LANES), jnp.float32),
            VMEM((2, STEPS * rows_all, 2 * LANES), jnp.float32),
            VMEM((2 * STEPS, LANES), jnp.float32),
            VMEM((1, LANES), jnp.float32),
            VMEM((2 * STEPS * 2 * rows_all, LANES), jnp.float32),
            VMEM((2, NFIELD, rows_all, LANES), jnp.float32),
            VMEM((2, STEPS, 2 * LANES), jnp.float32),
            VMEM((NFIELD, 2, LANES), jnp.float32),
            VMEM((1, LANES), jnp.float32),
            VMEM((freqs * PARTS * rows_all, LANES), jnp.float32),
            pltpu.SemaphoreType.DMA((6,)),
        ],
        cost_estimate=cost(20_000_000, 2_000_000),
        compiler_params=params(4096),
        name="finish",
    )(received, kron, held)
    return fields_out[None], spectra_out.reshape(spectra.shape), gradient


def solution(mesh):
    return jax.shard_map(
        program,
        mesh=mesh,
        in_specs=(
            P("role", None, "freq", "space"),
            P("role", "freq", None, None, "space"),
            P("freq"),
            P("freq"),
            P("freq", "space"),
            P(),
            P("role", None),
            P("role", None, None),
        ),
        out_specs=(
            P("role", None, "freq", "space"),
            P("role", "freq", None, None, "space"),
            P(("role", "freq"), "space"),
        ),
        check_vma=False,
    )
```

time: 50.1 us -> 38.6 us (0.77)
  Pallas kernels: 13.2 us -> 4.85 us
  waiting for transfers between devices: 4.3 us -> 11.3 us
  starting transfers between devices: 26.3 us -> 21.5 us
  local copies, waits for them, and re-layouts: 3.46 us -> 0.01 us
  other arithmetic: 1.56 us -> 0 us
    pallas_call x6 -> x4, Pallas kernels: 13.2 us -> 4.85 us  [the longest x1 2.44 us: program(): pl.pallas_call(functools.partial(finish, groups, freqs, count), out_shape...]
    all_to_all x2 -> x1, starting transfers between devices: 11.1 us -> 3.58 us  [program(): received = lax.all_to_all(message, ('role', 'freq'), 0, 0, tiled=True)]
    all_to_all x2 -> x1, waiting for transfers between devices: 4.3 us -> 8.33 us  [program(): received = lax.all_to_all(message, ('role', 'freq'), 0, 0, tiled=True)]
    ppermute x2, waiting for transfers between devices: 0.01 us -> 2.96 us  [the longest x1 2.95 us: program(): from_link = lax.ppermute(edge_link, 'space', swaps(size, 1))]
    ppermute x2, starting transfers between devices: 15.2 us -> 17.9 us  [the longest x1 16 us: program(): from_chip = lax.ppermute(edge_chip, 'space', swaps(size, 0))]
    unnamed x10 -> x2, local copies, waits for them, and re-layouts: 2.59 us -> 0.01 us
    convert_element_type x1 -> x0, other arithmetic: 1.53 us -> none  [phase_table(): return jnp.where(down % 8 == across % 8, value, 0.0).astype(jnp.bfloat16)]
    squeeze x1 -> x0, local copies, waits for them, and re-layouts: 0.72 us -> none  [local(): halo_high = lax.ppermute(edges[0], 'space', backward)]
  transfers between devices with their start and end apart: 4 -> 3, of which waited for: 1 -> 2; matrix products, arithmetic and copies ran while one was open for 5% -> 0% of each run, Pallas kernels for 20% -> 1%
where the time goes in v1:
time: 38.6 us; the launch traced here: 38.4 us
  starting transfers between devices  21.5 us (56%)
  waiting for transfers between devices  11.3 us (29%)
  Pallas kernels  4.85 us (13%)
  between operations  0.7 us (2%)
    ppermute x1, starting transfers between devices, program(): from_chip = lax.ppermute(edge_chip, 'space', swaps(size, 0))  16 us
    all_to_all x1, waiting for transfers between devices, program(): received = lax.all_to_all(message, ('role', 'freq'), 0, 0, tiled=True)  8.33 us
    all_to_all x1, starting transfers between devices, program(): received = lax.all_to_all(message, ('role', 'freq'), 0, 0, tiled=True)  3.58 us
    ppermute x1, waiting for transfers between devices, program(): from_link = lax.ppermute(edge_link, 'space', swaps(size, 1))  2.95 us
    pallas_call x1, Pallas kernels, program(): pl.pallas_call(functools.partial(finish, groups, freqs, count), out_shape...  2.44 us
    ppermute x1, starting transfers between devices, program(): from_link = lax.ppermute(edge_link, 'space', swaps(size, 1))  1.92 us
    pallas_call x1, Pallas kernels, program(): pl.pallas_call(functools.partial(pack_block, LANES * size), out_shape=[VM...  1.21 us
    pallas_call x1, Pallas kernels, program(): pl.pallas_call(functools.partial(pack_message, freqs), out_shape=jax.Shap...  0.98 us
  transfers between devices with their start and end apart: 3, of which 2 were waited for; matrix products, arithmetic and copies ran while one was open for 0% of the time, Pallas kernels for 1%

profile of v1, /device:TPU:1, one launch (start us, length us, event | category | flops | bytes accessed | tf_op | source)
XLA Modules:
  0.0 38.4 jit_solution(9314793067871125578)
XLA Ops:
  0.6 1.2 %pack_block.1 = (f32[24,128]{1,0:T(8,128)S(1)}, f32[2,128]{1,0:T(2,128)S(1)}, f32[2,128]{1,0:T(2,128)S(1)}, f32[1024,128]{1,0:T(8,128)S(1)}) custom-call(f32[5,2,128]{2,1,0:T(2,128)} %bitcast.10, s32[2,128]{1,0:T(2,128)} %ids_in.1, f32[3,8]{1,0:T(4,128)} %material_in.1, s32[1,16]{1,0:T(1,128)} %cells_in.1, s32[1,16]{1,0:T(1,128)} %bitcast.7, ...), custom_call_target="tpu_custom_call" | custom-call | flops 100000 | bytes 40000 | tf_op jit(solution)/shard_map/pack_block/pallas_call | solution.py:440
  1.9 16.0 %collective-permute-start = (f32[2,128]{1,0:T(2,128)S(1)}, f32[2,128]{1,0:T(2,128)S(1)}, u32[]{:S(2)}, u32[]{:S(2)}) collective-permute-start(f32[2,128]{1,0:T(2,128)S(1)} %get-tuple-element.11), channel_id=1, source_target_pairs={{0,8},{16,24},{32,40},{48,56},{64,72},{80,88},{96,104},{112,120},{... | collective-permute-start | bytes 3080 | tf_op jit(solution)/shard_map/ppermute | solution.py:477
  17.9 1.9 %collective-permute-start.1 = (f32[2,128]{1,0:T(2,128)S(1)}, f32[2,128]{1,0:T(2,128)S(1)}, u32[]{:S(2)}, u32[]{:S(2)}) collective-permute-start(f32[2,128]{1,0:T(2,128)S(1)} %get-tuple-element.12), channel_id=1, source_target_pairs={{8,16},{24,32},{40,48},{56,64},{72,80},{88,96},{104,112},{120,128}... | collective-permute-start | bytes 3080 | tf_op jit(solution)/shard_map/ppermute | solution.py:476
  19.8 0.0 collective-permute-done.from_chip
  19.8 3.0 %collective-permute-done.1.from_link = f32[2,128]{1,0:T(2,128)S(1)} collective-permute-done((f32[2,128]{1,0:T(2,128)S(1)}, f32[2,128]{1,0:T(2,128)S(1)}, u32[]{:S(2)}, u32[]{:S(2)}) %collective-permute-start.1) | collective-permute-done | bytes 1056 | tf_op jit(solution)/shard_map/ppermute | solution.py:476
  22.8 1.0 %pack_message.1 = bf16[16,112,128]{2,1,0:T(8,128)(2,1)} custom-call(f32[24,128]{1,0:T(8,128)S(1)} %get-tuple-element.10.block, f32[2,128]{1,0:T(2,128)S(1)} %collective-permute-done.from_chip, f32[2,128]{1,0:T(2,128)S(1)} %collective-permute-done.1.from_link, f32[1024,128]{1,0:T(8,128)S(1)} %get-tuple-element.13.spectra), custom_call_target="tpu_custom_call" | custom-call | flops 2000000 | bytes 1000000 | tf_op jit(solution)/shard_map/pack_message/pallas_call | solution.py:479
  23.8 0.0 copy-start
  23.8 3.6 %all-to-all-start = ((bf16[16,112,128]{2,1,0:T(8,128)(2,1)}), bf16[16,112,128]{2,1,0:T(8,128)(2,1)S(1)}, u32[]{:S(2)}, u32[]{:S(2)}) async-start(bf16[16,112,128]{2,1,0:T(8,128)(2,1)} %pack_message.1), calls=%async_computation | async-start | bytes 917504 | tf_op jit(solution)/shard_map/all_to_all | solution.py:492
  27.4 0.0 copy-done
  27.4 0.2 twiddle.1.kron
  27.6 8.3 %all-to-all-done.received = bf16[16,112,128]{2,1,0:T(8,128)(2,1)S(1)} async-done(((bf16[16,112,128]{2,1,0:T(8,128)(2,1)}), bf16[16,112,128]{2,1,0:T(8,128)(2,1)S(1)}, u32[]{:S(2)}, u32[]{:S(2)}) %all-to-all-start) | async-done | bytes 458784 | tf_op jit(solution)/shard_map/all_to_all | solution.py:492
  35.9 2.4 %finish.1 = (f32[5,2,128]{2,1,0:T(2,128)}, f32[1024,128]{1,0:T(8,128)}, f32[1,128]{1,0:T(1,128)}) custom-call(bf16[16,112,128]{2,1,0:T(8,128)(2,1)S(1)} %all-to-all-done.received, bf16[256,64]{1,0:T(8,128)(2,1)S(1)} %twiddle.1.kron, f32[1024,128]{1,0:T(8,128)S(1)} %get-tuple-element.13.spectra), custom_call_target="tpu_custom_call" | custom-call | flops 20000000 | bytes 2000000 | tf_op jit(solution)/shard_map/finish/pallas_call | solution.py:504
Async XLA Ops:
  1.9 18.0 %collective-permute-start = (f32[2,128]{1,0:T(2,128)S(1)}, f32[2,128]{1,0:T(2,128)S(1)}, u32[]{:S(2)}, u32[]{:S(2)}) collective-permute-start(f32[2,128]{1,0:T(2,128)S(1)} %get-tuple-element.11), channel_id=1, source_target_pairs={{0,8},{16,24},{32,40},{48,56},{64,72},{80,88},{96,104},{112,120},{... | collective-permute-start | bytes 3080 | tf_op jit(solution)/shard_map/ppermute | solution.py:477
  17.9 4.9 %collective-permute-start.1 = (f32[2,128]{1,0:T(2,128)S(1)}, f32[2,128]{1,0:T(2,128)S(1)}, u32[]{:S(2)}, u32[]{:S(2)}) collective-permute-start(f32[2,128]{1,0:T(2,128)S(1)} %get-tuple-element.12), channel_id=1, source_target_pairs={{8,16},{24,32},{40,48},{56,64},{72,80},{88,96},{104,112},{120,128}... | collective-permute-start | bytes 3080 | tf_op jit(solution)/shard_map/ppermute | solution.py:476
  23.8 3.6 %copy-start = (s32[16]{0:T(128)S(1)}, s32[16]{0:T(128)}, u32[]{:S(2)}) copy-start(s32[16]{0:T(128)} %param.10) | copy-start | bytes 196
  23.8 12.1 %all-to-all-start = ((bf16[16,112,128]{2,1,0:T(8,128)(2,1)}), bf16[16,112,128]{2,1,0:T(8,128)(2,1)S(1)}, u32[]{:S(2)}, u32[]{:S(2)}) async-start(bf16[16,112,128]{2,1,0:T(8,128)(2,1)} %pack_message.1), calls=%async_computation | async-start | bytes 917504 | tf_op jit(solution)/shard_map/all_to_all | solution.py:492

commit v2 on v1

--- a/solution.py
+++ b/solution.py
@@ -120,36 +120,34 @@
     copies[-1].wait()
 
 
-def pack_message(freqs, block, from_chip, from_link, spectra, message, built, sems):
+def pack_spectra(freqs, spectra, message):
     rows_all = message.shape[0]
+    for row in range(rows_all):
+        for part in range(PARTS):
+            picked = spectra[pl.ds(part * rows_all + row, freqs, stride=PARTS * rows_all), :]
+            message[row, part * freqs : (part + 1) * freqs, :] = picked.astype(jnp.bfloat16)
+
+
+def pack_rows(block, from_chip, from_link, row_spectra, message, tile):
     even = is_even()
     before = jnp.where(even, from_link[...], from_chip[...])
     after = jnp.where(even, from_chip[...], from_link[...])
-    block[ROW_HALO : ROW_HALO + 2, :] = before + pltpu.roll(after, LANES // 2, 1)
-    exact = block[...]
+    tile[...] = block[...]
+    tile[ROW_HALO : ROW_HALO + 2, :] = before + pltpu.roll(after, LANES // 2, 1)
+    exact = tile[...]
     high = exact.astype(jnp.bfloat16).astype(jnp.float32)
     both = jnp.concatenate([high, exact - high], axis=0).astype(jnp.bfloat16)
-    copies = []
-    for row in range(rows_all):
-        built[row, : 2 * MSG_ROWS, :] = both
-        for part in range(PARTS):
-            picked = spectra[pl.ds(part * rows_all + row, freqs, stride=PARTS * rows_all), :]
-            first = 2 * MSG_ROWS + part * freqs
-            built[row, first : first + freqs, :] = picked.astype(jnp.bfloat16)
-        if row % 4 == 3:
-            span = pl.ds(row - 3, 4)
-            copy = pltpu.make_async_copy(built.at[span], message.at[span], sems.at[row // 4])
-            copy.start()
-            copies.append(copy)
-    for copy in copies:
-        copy.wait()
-
-
-def twiddle(freqs, index, kron):
+    for row in range(message.shape[0]):
+        message[row, : 2 * MSG_ROWS, :] = both
+        message[row, 2 * MSG_ROWS :, :] = row_spectra[row]
+
+
+def twiddle(freqs, block, kron):
     span = 8 * STEPS
     lanes = lax.broadcasted_iota(jnp.int32, (freqs, freqs), 1)
     rows = lax.broadcasted_iota(jnp.int32, (freqs, freqs), 0)
-    diagonal = jnp.where(lanes == rows, index[...].astype(jnp.float32), 0.0)
+    index = block[ROW_INDEX : ROW_INDEX + 1, :freqs]
+    diagonal = jnp.where(lanes == rows, index, 0.0)
     column = jnp.sum(diagonal, axis=1, keepdims=True).astype(jnp.int32)
     across = lax.bitwise_and(lane_ids((freqs, 2 * span)), span - 1)
     turns = lax.bitwise_and(column * lax.shift_right_logical(across, 3), PERIOD - 1)
@@ -476,21 +474,6 @@
     from_link = lax.ppermute(edge_link, "space", swaps(size, 1))
     from_chip = lax.ppermute(edge_chip, "space", swaps(size, 0))
 
-    message = pl.pallas_call(
-        functools.partial(pack_message, freqs),
-        out_shape=jax.ShapeDtypeStruct((members, message_rows, LANES), jnp.bfloat16),
-        in_specs=[whole()] * 4,
-        out_specs=whole(pl.ANY),
-        scratch_shapes=[
-            VMEM((members, message_rows, LANES), jnp.bfloat16),
-            pltpu.SemaphoreType.DMA((members // 4,)),
-        ],
-        cost_estimate=cost(2_000_000, 1_000_000),
-        compiler_params=params(1536),
-        name="pack_message",
-    )(block, from_chip, from_link, held)
-    received = lax.all_to_all(message, ("role", "freq"), 0, 0, tiled=True)
-
     kron = pl.pallas_call(
         functools.partial(twiddle, freqs),
         out_shape=jax.ShapeDtypeStruct((freqs * 16, STEPS * 8), jnp.bfloat16),
@@ -499,7 +482,28 @@
         cost_estimate=cost(100_000, 40_000),
         compiler_params=params(512),
         name="twiddle",
-    )(freq_index[None])
+    )(block)
+
+    row_spectra = pl.pallas_call(
+        functools.partial(pack_spectra, freqs),
+        out_shape=VMEM((members, PARTS * freqs, LANES), jnp.bfloat16),
+        in_specs=[whole()],
+        out_specs=whole(),
+        cost_estimate=cost(2_000_000, 1_000_000),
+        compiler_params=params(1536),
+        name="pack_spectra",
+    )(held)
+    message = pl.pallas_call(
+        pack_rows,
+        out_shape=VMEM((members, message_rows, LANES), jnp.bfloat16),
+        in_specs=[whole()] * 4,
+        out_specs=whole(),
+        scratch_shapes=[VMEM((MSG_ROWS, LANES), jnp.float32)],
+        cost_estimate=cost(100_000, 300_000),
+        compiler_params=params(2048),
+        name="pack_rows",
+    )(block, from_chip, from_link, row_spectra)
+    received = lax.all_to_all(message, ("role", "freq"), 0, 0, tiled=True)
 
     fields_out, spectra_out, gradient = pl.pallas_call(
         functools.partial(finish, groups, freqs, count),

time: 38.6 us -> 38.5 us (level)
    pallas_call x1 -> x2, Pallas kernels: 0.98 us -> 1.16 us  [the longest x1 0.87 us: program(): pl.pallas_call(pack_rows, out_shape=VMEM((members, message_rows, LANES),...]
where the time goes in v2:
time: 38.5 us; the launch traced here: 38.2 us
  starting transfers between devices  21.5 us (56%)
  waiting for transfers between devices  11 us (29%)
  Pallas kernels  5.02 us (13%)
  between operations  0.69 us (2%)
    ppermute x1, starting transfers between devices, program(): from_chip = lax.ppermute(edge_chip, 'space', swaps(size, 0))  16 us
    all_to_all x1, waiting for transfers between devices, program(): received = lax.all_to_all(message, ('role', 'freq'), 0, 0, tiled=True)  8.34 us
    all_to_all x1, starting transfers between devices, program(): received = lax.all_to_all(message, ('role', 'freq'), 0, 0, tiled=True)  3.56 us
    ppermute x1, waiting for transfers between devices, program(): from_link = lax.ppermute(edge_link, 'space', swaps(size, 1))  2.65 us
    pallas_call x1, Pallas kernels, program(): pl.pallas_call(functools.partial(finish, groups, freqs, count), out_shape...  2.44 us
    ppermute x1, starting transfers between devices, program(): from_link = lax.ppermute(edge_link, 'space', swaps(size, 1))  1.92 us
    pallas_call x1, Pallas kernels, program(): pl.pallas_call(functools.partial(pack_block, LANES * size), out_shape=[VM...  1.21 us
    pallas_call x1, Pallas kernels, program(): pl.pallas_call(pack_rows, out_shape=VMEM((members, message_rows, LANES),...  0.87 us
  transfers between devices with their start and end apart: 3, of which 2 were waited for; matrix products, arithmetic and copies ran while one was open for 0% of the time, Pallas kernels for 1%

profile of v2, /device:TPU:1, one launch (start us, length us, event | category | flops | bytes accessed | tf_op | source)
XLA Modules:
  0.0 38.2 jit_solution(8422115487989052044)
XLA Ops:
  0.6 1.2 %pack_block.1 = (f32[24,128]{1,0:T(8,128)S(1)}, f32[2,128]{1,0:T(2,128)S(1)}, f32[2,128]{1,0:T(2,128)S(1)}, f32[1024,128]{1,0:T(8,128)S(1)}) custom-call(f32[5,2,128]{2,1,0:T(2,128)} %bitcast.8, s32[2,128]{1,0:T(2,128)} %ids_in.1, f32[3,8]{1,0:T(4,128)} %material_in.1, s32[1,16]{1,0:T(1,128)} %cells_in.1, s32[1,16]{1,0:T(1,128)} %bitcast.10, ...), custom_call_target="tpu_custom_call" | custom-call | flops 100000 | bytes 40000 | tf_op jit(solution)/shard_map/pack_block/pallas_call | solution.py:438
  1.9 16.0 %collective-permute-start = (f32[2,128]{1,0:T(2,128)S(1)}, f32[2,128]{1,0:T(2,128)S(1)}, u32[]{:S(2)}, u32[]{:S(2)}) collective-permute-start(f32[2,128]{1,0:T(2,128)S(1)} %get-tuple-element.11), channel_id=1, source_target_pairs={{0,8},{16,24},{32,40},{48,56},{64,72},{80,88},{96,104},{112,120},{... | collective-permute-start | bytes 3080 | tf_op jit(solution)/shard_map/ppermute | solution.py:475
  17.9 1.9 %collective-permute-start.1 = (f32[2,128]{1,0:T(2,128)S(1)}, f32[2,128]{1,0:T(2,128)S(1)}, u32[]{:S(2)}, u32[]{:S(2)}) collective-permute-start(f32[2,128]{1,0:T(2,128)S(1)} %get-tuple-element.12), channel_id=1, source_target_pairs={{8,16},{24,32},{40,48},{56,64},{72,80},{88,96},{104,112},{120,128}... | collective-permute-start | bytes 3080 | tf_op jit(solution)/shard_map/ppermute | solution.py:474
  19.8 0.3 pack_spectra.1.row_spectra
  20.1 0.0 collective-permute-done.from_chip
  20.1 2.7 %collective-permute-done.1.from_link = f32[2,128]{1,0:T(2,128)S(1)} collective-permute-done((f32[2,128]{1,0:T(2,128)S(1)}, f32[2,128]{1,0:T(2,128)S(1)}, u32[]{:S(2)}, u32[]{:S(2)}) %collective-permute-start.1) | collective-permute-done | bytes 1056 | tf_op jit(solution)/shard_map/ppermute | solution.py:474
  22.8 0.9 %pack_rows.1 = bf16[16,112,128]{2,1,0:T(8,128)(2,1)} custom-call(f32[24,128]{1,0:T(8,128)S(1)} %get-tuple-element.10.block, f32[2,128]{1,0:T(2,128)S(1)} %collective-permute-done.from_chip, f32[2,128]{1,0:T(2,128)S(1)} %collective-permute-done.1.from_link, bf16[16,64,128]{2,1,0:T(8,128)(2,1)S(1)} %pack_spectra.1.row_spectra), custom_call_target="tpu_custom_call" | custom-call | flops 100000 | bytes 300000 | tf_op jit(solution)/shard_map/pack_rows/pallas_call | solution.py:496
  23.6 3.6 %all-to-all-start = ((bf16[16,112,128]{2,1,0:T(8,128)(2,1)}), bf16[16,112,128]{2,1,0:T(8,128)(2,1)S(1)}, u32[]{:S(2)}, u32[]{:S(2)}) async-start(bf16[16,112,128]{2,1,0:T(8,128)(2,1)} %pack_rows.1), calls=%async_computation | async-start | bytes 917504 | tf_op jit(solution)/shard_map/all_to_all | solution.py:506
  27.2 0.2 twiddle.1.kron
  27.4 8.3 %all-to-all-done.received = bf16[16,112,128]{2,1,0:T(8,128)(2,1)S(1)} async-done(((bf16[16,112,128]{2,1,0:T(8,128)(2,1)}), bf16[16,112,128]{2,1,0:T(8,128)(2,1)S(1)}, u32[]{:S(2)}, u32[]{:S(2)}) %all-to-all-start) | async-done | bytes 458784 | tf_op jit(solution)/shard_map/all_to_all | solution.py:506
  35.8 2.4 %finish.1 = (f32[5,2,128]{2,1,0:T(2,128)}, f32[1024,128]{1,0:T(8,128)}, f32[1,128]{1,0:T(1,128)}) custom-call(bf16[16,112,128]{2,1,0:T(8,128)(2,1)S(1)} %all-to-all-done.received, bf16[256,64]{1,0:T(8,128)(2,1)S(1)} %twiddle.1.kron, f32[1024,128]{1,0:T(8,128)S(1)} %get-tuple-element.13.spectra), custom_call_target="tpu_custom_call" | custom-call | flops 20000000 | bytes 2000000 | tf_op jit(solution)/shard_map/finish/pallas_call | solution.py:508
Async XLA Ops:
  1.9 18.3 %collective-permute-start = (f32[2,128]{1,0:T(2,128)S(1)}, f32[2,128]{1,0:T(2,128)S(1)}, u32[]{:S(2)}, u32[]{:S(2)}) collective-permute-start(f32[2,128]{1,0:T(2,128)S(1)} %get-tuple-element.11), channel_id=1, source_target_pairs={{0,8},{16,24},{32,40},{48,56},{64,72},{80,88},{96,104},{112,120},{... | collective-permute-start | bytes 3080 | tf_op jit(solution)/shard_map/ppermute | solution.py:475
  17.9 4.9 %collective-permute-start.1 = (f32[2,128]{1,0:T(2,128)S(1)}, f32[2,128]{1,0:T(2,128)S(1)}, u32[]{:S(2)}, u32[]{:S(2)}) collective-permute-start(f32[2,128]{1,0:T(2,128)S(1)} %get-tuple-element.12), channel_id=1, source_target_pairs={{8,16},{24,32},{40,48},{56,64},{72,80},{88,96},{104,112},{120,128}... | collective-permute-start | bytes 3080 | tf_op jit(solution)/shard_map/ppermute | solution.py:474
  23.6 12.1 %all-to-all-start = ((bf16[16,112,128]{2,1,0:T(8,128)(2,1)}), bf16[16,112,128]{2,1,0:T(8,128)(2,1)S(1)}, u32[]{:S(2)}, u32[]{:S(2)}) async-start(bf16[16,112,128]{2,1,0:T(8,128)(2,1)} %pack_rows.1), calls=%async_computation | async-start | bytes 917504 | tf_op jit(solution)/shard_map/all_to_all | solution.py:506

commit v3 on v2

--- a/solution.py
+++ b/solution.py
@@ -19,14 +19,14 @@
 LANES = 128
 HALO = STEPS
 PARTS = 4
-CHANNELS = NFIELD + NPROP
+CHANNELS = NFIELD + 1
+ROW_IDS = 2 * NFIELD
 ROW_HALO = 2 * CHANNELS
-ROW_CELL_ROW = 18
-ROW_CELL_COLUMN = 19
-ROW_INDEX = 20
-ROW_WEIGHT = 21
-ROW_WAVELET = 22
-MSG_ROWS = 24
+ROW_LISTS = 14
+ROW_WAVELET = 15
+MSG_ROWS = 16
+LIST = 16
+AT_CELL_ROW, AT_CELL_COLUMN, AT_INDEX, AT_WEIGHT = (LIST * slot for slot in range(4))
 VMEM = pltpu.VMEM
 
 
@@ -64,6 +64,7 @@
     edge_chip,
     edge_link,
     spectra,
+    shades,
     fields,
     ids,
     material,
@@ -88,23 +89,22 @@
         copy.wait()
     for field in range(NFIELD):
         block[2 * field : 2 * field + 2, :] = fields[field]
-    which = ids[...]
+    block[ROW_IDS : ROW_IDS + 2, :] = (ids[...] + 1).astype(jnp.float32)
     for prop in range(NPROP):
-        value = jnp.zeros(which.shape, jnp.float32)
         for kind in range(NMAT):
-            value = jnp.where(which == kind, material[prop, kind], value)
-        row = 2 * (NFIELD + prop)
-        block[row : row + 2, :] = COURANT * value
-    count = cells.shape[1]
+            value = jnp.full((1, LANES), COURANT * material[prop, kind], jnp.float32)
+            row = prop * NMAT + kind
+            shades[row : row + 1, :] = value
     cell_row = lax.div(cells[...], width_all)
-    block[ROW_CELL_ROW : ROW_CELL_ROW + 1, :count] = cell_row.astype(jnp.float32)
     cell_column = cells[...] - cell_row * width_all
-    block[ROW_CELL_COLUMN : ROW_CELL_COLUMN + 1, :count] = cell_column.astype(jnp.float32)
-    block[ROW_INDEX : ROW_INDEX + 1, : index.shape[1]] = index[...].astype(jnp.float32)
-    block[ROW_WEIGHT : ROW_WEIGHT + 1, : weight.shape[1]] = weight[...]
-    wide[:, :count] = wavelets[...]
-    spread = pltpu.roll(wide[...], 0, 1, stride=count, stride_axis=0)
-    block[ROW_WAVELET : ROW_WAVELET + 1, :] = jnp.sum(spread, axis=0, keepdims=True)
+    wide[:STEPS, :LIST] = wavelets[...]
+    lists = (cell_row.astype(jnp.float32), cell_column.astype(jnp.float32))
+    lists += (index[...].astype(jnp.float32), weight[...])
+    for slot, value in enumerate(lists):
+        wide[STEPS + slot : STEPS + slot + 1, :LIST] = value
+    for row, first in ((ROW_WAVELET, 0), (ROW_LISTS, STEPS)):
+        spread = pltpu.roll(wide[first : first + 8, :], 0, 1, stride=LIST, stride_axis=0)
+        block[row : row + 1, :] = jnp.sum(spread, axis=0, keepdims=True)
     lanes = lane_ids((2, LANES))
     low = jnp.zeros((2, LANES), jnp.float32)
     high = jnp.zeros((2, LANES), jnp.float32)
@@ -146,7 +146,7 @@
     span = 8 * STEPS
     lanes = lax.broadcasted_iota(jnp.int32, (freqs, freqs), 1)
     rows = lax.broadcasted_iota(jnp.int32, (freqs, freqs), 0)
-    index = block[ROW_INDEX : ROW_INDEX + 1, :freqs]
+    index = pltpu.roll(block[ROW_LISTS : ROW_LISTS + 1, :], LANES - AT_INDEX, 1)[:, :freqs]
     diagonal = jnp.where(lanes == rows, index, 0.0)
     column = jnp.sum(diagonal, axis=1, keepdims=True).astype(jnp.int32)
     across = lax.bitwise_and(lane_ids((freqs, 2 * span)), span - 1)
@@ -184,21 +184,22 @@
         for field in range(NFIELD):
             gather(center, (role * NFIELD + field) * rows_all, role, 2 * field)
         gather(halos, role * rows_all, role, ROW_HALO)
-    for prop in range(NPROP):
-        gather(center, (2 * NFIELD + prop) * rows_all, 0, 2 * (NFIELD + prop))
-
-
-def prepare(groups, freqs, count, decoded, inject, table, weights):
+    gather(center, 2 * NFIELD * rows_all, 0, ROW_IDS)
+
+
+def prepare(groups, count, decoded, inject, table, weights):
     rows_all = 2 * groups
     first_column = lax.axis_index("space") * LANES
 
-    def joined(row):
-        value = decoded[pl.ds(row, groups, stride=MSG_ROWS), :]
-        spread = pltpu.roll(value, 0, 1, stride=freqs, stride_axis=0)
+    def joined(first):
+        value = decoded[pl.ds(ROW_LISTS, groups, stride=MSG_ROWS), :]
+        value = pltpu.roll(value, LANES - first, 1)
+        value = jnp.where(lane_ids((groups, LANES)) < LIST, value, 0.0)
+        spread = pltpu.roll(value, 0, 1, stride=LIST, stride_axis=0)
         return jnp.sum(spread, axis=0, keepdims=True)
 
-    weights[...] = joined(ROW_WEIGHT)
-    index = joined(ROW_INDEX).astype(jnp.int32)
+    weights[...] = joined(AT_WEIGHT)
+    index = joined(AT_INDEX).astype(jnp.int32)
     times = lax.broadcasted_iota(jnp.int32, (STEPS, LANES), 0)
     turns = lax.bitwise_and(index * times, PERIOD - 1)
     angle = turns.astype(jnp.float32) * (TWO_PI / PERIOD)
@@ -210,14 +211,16 @@
     lanes = lane_ids((rows_all, LANES))
     row_lanes = lane_ids((1, LANES))
 
-    def twice(row):
-        value = jnp.where(row_lanes < count, row, 0.0)
+    def twice(row, first):
+        value = pltpu.roll(row, (LANES - first) % LANES, 1)
+        value = jnp.where(row_lanes < count, value, 0.0)
         return value + pltpu.roll(value, count, 1)
 
     for role in range(2):
         base = role * groups * MSG_ROWS
-        cell_row = twice(decoded[base + ROW_CELL_ROW : base + ROW_CELL_ROW + 1, :])
-        cell_column = twice(decoded[base + ROW_CELL_COLUMN : base + ROW_CELL_COLUMN + 1, :])
+        lists = decoded[base + ROW_LISTS : base + ROW_LISTS + 1, :]
+        cell_row = twice(lists, AT_CELL_ROW)
+        cell_column = twice(lists, AT_CELL_COLUMN)
         near = cell_column.astype(jnp.int32) - first_column
         hit_column = jnp.where(window == near, 1.0, 0.0).astype(jnp.bfloat16)
         hit_row = jnp.logical_and(row_ids == cell_row.astype(jnp.int32), lanes < 2 * count)
@@ -236,7 +239,7 @@
         )
 
 
-def step_fields(groups, center, halos, inject, snaps, finals):
+def step_fields(groups, center, halos, shades, inject, snaps, finals):
     rows_all = 2 * groups
     lanes = lane_ids((rows_all, LANES))
     row_ids = lax.broadcasted_iota(jnp.int32, (rows_all, 2 * LANES), 0)
@@ -261,9 +264,17 @@
     def before(value):
         return pltpu.roll(value, 1, 1)
 
-    buoyancy, lame_first, lame_second = (
-        extended(2 * NFIELD + prop, 0, NFIELD + prop) for prop in range(NPROP)
-    )
+    which = extended(2 * NFIELD, 0, NFIELD)
+    props = []
+    for prop in range(NPROP):
+        value = jnp.zeros_like(which)
+        for kind in range(NMAT):
+            row = prop * NMAT + kind
+            shade = shades[row : row + 1, :]
+            shade = jnp.broadcast_to(jnp.concatenate([shade, shade], axis=1), which.shape)
+            value = jnp.where(which == kind + 1.0, shade, value)
+        props.append(value)
+    buoyancy, lame_first, lame_second = props
     stiff = lame_first + 2.0 * lame_second
     for role in range(2):
         vel_x, vel_z, sig_xx, sig_zz, sig_xz = (
@@ -335,6 +346,7 @@
     received,
     kron,
     spectra,
+    shades,
     fields_out,
     spectra_out,
     gradient_out,
@@ -356,8 +368,8 @@
     own_role = lax.axis_index("role")
     own_group = lax.axis_index("freq")
     unpack(groups, received, decoded, center, halos)
-    prepare(groups, freqs, count, decoded, inject, table, weights)
-    step_fields(groups, center, halos, inject, snaps, finals)
+    prepare(groups, count, decoded, inject, table, weights)
+    step_fields(groups, center, halos, shades, inject, snaps, finals)
     for field in range(NFIELD):
         own_fields[field] = finals[own_role, field, pl.ds(2 * own_group, 2), :]
     copies = [pltpu.make_async_copy(own_fields, fields_out, sems.at[0])]
@@ -435,16 +447,17 @@
     flat = spectra.reshape(freqs * PARTS * rows_all, LANES)
     message_rows = 2 * MSG_ROWS + PARTS * freqs
 
-    block, edge_chip, edge_link, held = pl.pallas_call(
+    block, edge_chip, edge_link, held, shades = pl.pallas_call(
         functools.partial(pack_block, LANES * size),
         out_shape=[
             VMEM((MSG_ROWS, LANES), jnp.float32),
             VMEM((2, LANES), jnp.float32),
             VMEM((2, LANES), jnp.float32),
             VMEM(flat.shape, jnp.float32),
+            VMEM((NPROP * NMAT, LANES), jnp.float32),
         ],
         in_specs=[whole(pl.ANY)] * 8,
-        out_specs=[whole()] * 4,
+        out_specs=[whole()] * 5,
         scratch_shapes=[
             VMEM((NFIELD, 2, LANES), jnp.float32),
             VMEM((2, LANES), jnp.int32),
@@ -453,7 +466,7 @@
             VMEM((1, freqs), jnp.int32),
             VMEM((1, freqs), jnp.float32),
             VMEM((STEPS, count), jnp.float32),
-            VMEM((STEPS, LANES), jnp.float32),
+            VMEM((2 * STEPS, LANES), jnp.float32),
             pltpu.SemaphoreType.DMA((8,)),
         ],
         cost_estimate=cost(100_000, 40_000),
@@ -512,11 +525,11 @@
             f32(freqs * PARTS * rows_all, LANES),
             f32(1, LANES),
         ],
-        in_specs=[whole()] * 3,
+        in_specs=[whole()] * 4,
         out_specs=[whole(pl.ANY)] * 3,
         scratch_shapes=[
             VMEM((members * MSG_ROWS, LANES), jnp.float32),
-            VMEM(((2 * NFIELD + NPROP) * rows_all, LANES), jnp.float32),
+            VMEM(((2 * NFIELD + 1) * rows_all, LANES), jnp.float32),
             VMEM((2 * rows_all, LANES), jnp.float32),
             VMEM((2, STEPS * rows_all, 2 * LANES), jnp.float32),
             VMEM((2 * STEPS, LANES), jnp.float32),
@@ -532,7 +545,7 @@
         cost_estimate=cost(20_000_000, 2_000_000),
         compiler_params=params(4096),
         name="finish",
-    )(received, kron, held)
+    )(received, kron, held, shades)
     return fields_out[None], spectra_out.reshape(spectra.shape), gradient
 
 

time: 38.5 us -> 38.2 us (level)
  waiting for transfers between devices: 11 us -> 10.6 us
    all_to_all x1, waiting for transfers between devices: 8.34 us -> 7.92 us  [program(): received = lax.all_to_all(message, ('role', 'freq'), 0, 0, tiled=True)]
  transfers between devices with their start and end apart: 3 -> 3, of which waited for: 2 -> 2; matrix products, arithmetic and copies ran while one was open for 0% -> 0% of each run, Pallas kernels for 1% -> 2%
where the time goes in v3:
time: 38.2 us; the launch traced here: 37.9 us
  starting transfers between devices  21.5 us (56%)
  waiting for transfers between devices  10.6 us (28%)
  Pallas kernels  5.17 us (14%)
  between operations  0.69 us (2%)
    ppermute x1, starting transfers between devices, program(): from_chip = lax.ppermute(edge_chip, 'space', swaps(size, 0))  16 us
    all_to_all x1, waiting for transfers between devices, program(): received = lax.all_to_all(message, ('role', 'freq'), 0, 0, tiled=True)  7.92 us
    all_to_all x1, starting transfers between devices, program(): received = lax.all_to_all(message, ('role', 'freq'), 0, 0, tiled=True)  3.55 us
    ppermute x1, waiting for transfers between devices, program(): from_link = lax.ppermute(edge_link, 'space', swaps(size, 1))  2.65 us
    pallas_call x1, Pallas kernels, program(): pl.pallas_call(functools.partial(finish, groups, freqs, count), out_shape...  2.54 us
    ppermute x1, starting transfers between devices, program(): from_link = lax.ppermute(edge_link, 'space', swaps(size, 1))  1.92 us
    pallas_call x1, Pallas kernels, program(): pl.pallas_call(functools.partial(pack_block, LANES * size), out_shape=[VM...  1.21 us
    pallas_call x1, Pallas kernels, program(): pl.pallas_call(pack_rows, out_shape=VMEM((members, message_rows, LANES),...  0.85 us
  transfers between devices with their start and end apart: 3, of which 2 were waited for; matrix products, arithmetic and copies ran while one was open for 0% of the time, Pallas kernels for 2%

profile of v3, /device:TPU:1, one launch (start us, length us, event | category | flops | bytes accessed | tf_op | source)
XLA Modules:
  0.0 37.9 jit_solution(10195851663020917246)
XLA Ops:
  0.6 1.2 %pack_block.1 = (f32[16,128]{1,0:T(8,128)S(1)}, f32[2,128]{1,0:T(2,128)S(1)}, f32[2,128]{1,0:T(2,128)S(1)}, f32[1024,128]{1,0:T(8,128)S(1)}, f32[24,128]{1,0:T(8,128)S(1)}) custom-call(f32[5,2,128]{2,1,0:T(2,128)} %bitcast.8, s32[2,128]{1,0:T(2,128)} %ids_in.1, f32[3,8]{1,0:T(4,128)} %material_in.1, s32[1,16]{1,0:T(1,128)} %cells_in.1, s32[1,16]{1,0:T(1,128)} %bitcast.10, ...), custom_call_target="tpu_custom_call" | custom-call | flops 100000 | bytes 40000 | tf_op jit(solution)/shard_map/pack_block/pallas_call | solution.py:450
  1.9 16.0 %collective-permute-start = (f32[2,128]{1,0:T(2,128)S(1)}, f32[2,128]{1,0:T(2,128)S(1)}, u32[]{:S(2)}, u32[]{:S(2)}) collective-permute-start(f32[2,128]{1,0:T(2,128)S(1)} %get-tuple-element.12), channel_id=1, source_target_pairs={{0,8},{16,24},{32,40},{48,56},{64,72},{80,88},{96,104},{112,120},{... | collective-permute-start | bytes 3080 | tf_op jit(solution)/shard_map/ppermute | solution.py:488
  17.9 1.9 %collective-permute-start.1 = (f32[2,128]{1,0:T(2,128)S(1)}, f32[2,128]{1,0:T(2,128)S(1)}, u32[]{:S(2)}, u32[]{:S(2)}) collective-permute-start(f32[2,128]{1,0:T(2,128)S(1)} %get-tuple-element.13), channel_id=1, source_target_pairs={{8,16},{24,32},{40,48},{56,64},{72,80},{88,96},{104,112},{120,128}... | collective-permute-start | bytes 3080 | tf_op jit(solution)/shard_map/ppermute | solution.py:487
  19.8 0.3 pack_spectra.1.row_spectra
  20.1 0.0 collective-permute-done.from_chip
  20.1 2.7 %collective-permute-done.1.from_link = f32[2,128]{1,0:T(2,128)S(1)} collective-permute-done((f32[2,128]{1,0:T(2,128)S(1)}, f32[2,128]{1,0:T(2,128)S(1)}, u32[]{:S(2)}, u32[]{:S(2)}) %collective-permute-start.1) | collective-permute-done | bytes 1056 | tf_op jit(solution)/shard_map/ppermute | solution.py:487
  22.8 0.8 %pack_rows.1 = bf16[16,96,128]{2,1,0:T(8,128)(2,1)} custom-call(f32[16,128]{1,0:T(8,128)S(1)} %get-tuple-element.11.block, f32[2,128]{1,0:T(2,128)S(1)} %collective-permute-done.from_chip, f32[2,128]{1,0:T(2,128)S(1)} %collective-permute-done.1.from_link, bf16[16,64,128]{2,1,0:T(8,128)(2,1)S(1)} %pack_spectra.1.row_spectra), custom_call_target="tpu_custom_call" | custom-call | flops 100000 | bytes 300000 | tf_op jit(solution)/shard_map/pack_rows/pallas_call | solution.py:509
  23.6 3.6 %all-to-all-start = ((bf16[16,96,128]{2,1,0:T(8,128)(2,1)}), bf16[16,96,128]{2,1,0:T(8,128)(2,1)S(1)}, u32[]{:S(2)}, u32[]{:S(2)}) async-start(bf16[16,96,128]{2,1,0:T(8,128)(2,1)} %pack_rows.1), calls=%async_computation | async-start | bytes 786432 | tf_op jit(solution)/shard_map/all_to_all | solution.py:519
  27.2 0.3 twiddle.1.kron
  27.5 7.9 %all-to-all-done.received = bf16[16,96,128]{2,1,0:T(8,128)(2,1)S(1)} async-done(((bf16[16,96,128]{2,1,0:T(8,128)(2,1)}), bf16[16,96,128]{2,1,0:T(8,128)(2,1)S(1)}, u32[]{:S(2)}, u32[]{:S(2)}) %all-to-all-start) | async-done | bytes 393248 | tf_op jit(solution)/shard_map/all_to_all | solution.py:519
  35.4 2.5 %finish.1 = (f32[5,2,128]{2,1,0:T(2,128)}, f32[1024,128]{1,0:T(8,128)}, f32[1,128]{1,0:T(1,128)}) custom-call(bf16[16,96,128]{2,1,0:T(8,128)(2,1)S(1)} %all-to-all-done.received, bf16[256,64]{1,0:T(8,128)(2,1)S(1)} %twiddle.1.kron, f32[1024,128]{1,0:T(8,128)S(1)} %get-tuple-element.14.spectra, f32[24,128]{1,0:T(8,128)S(1)} %get-tuple-element.15.shades), custom_call_target="tpu_custom_call" | custom-call | flops 20000000 | bytes 2000000 | tf_op jit(solution)/shard_map/finish/pallas_call | solution.py:521
Async XLA Ops:
  1.9 18.3 %collective-permute-start = (f32[2,128]{1,0:T(2,128)S(1)}, f32[2,128]{1,0:T(2,128)S(1)}, u32[]{:S(2)}, u32[]{:S(2)}) collective-permute-start(f32[2,128]{1,0:T(2,128)S(1)} %get-tuple-element.12), channel_id=1, source_target_pairs={{0,8},{16,24},{32,40},{48,56},{64,72},{80,88},{96,104},{112,120},{... | collective-permute-start | bytes 3080 | tf_op jit(solution)/shard_map/ppermute | solution.py:488
  17.9 4.9 %collective-permute-start.1 = (f32[2,128]{1,0:T(2,128)S(1)}, f32[2,128]{1,0:T(2,128)S(1)}, u32[]{:S(2)}, u32[]{:S(2)}) collective-permute-start(f32[2,128]{1,0:T(2,128)S(1)} %get-tuple-element.13), channel_id=1, source_target_pairs={{8,16},{24,32},{40,48},{56,64},{72,80},{88,96},{104,112},{120,128}... | collective-permute-start | bytes 3080 | tf_op jit(solution)/shard_map/ppermute | solution.py:487
  23.6 11.8 %all-to-all-start = ((bf16[16,96,128]{2,1,0:T(8,128)(2,1)}), bf16[16,96,128]{2,1,0:T(8,128)(2,1)S(1)}, u32[]{:S(2)}, u32[]{:S(2)}) async-start(bf16[16,96,128]{2,1,0:T(8,128)(2,1)} %pack_rows.1), calls=%async_computation | async-start | bytes 786432 | tf_op jit(solution)/shard_map/all_to_all | solution.py:519

commit v4 on v3

--- a/solution.py
+++ b/solution.py
@@ -176,7 +176,7 @@
     def gather(target, at, role, first):
         for k in range(2):
             start = role * groups * MSG_ROWS + first + k
-            target[pl.ds(at + k, groups, stride=2), :] = decoded[
+            target[at + k * groups : at + (k + 1) * groups, :] = decoded[
                 pl.ds(start, groups, stride=MSG_ROWS), :
             ]
 
@@ -206,8 +206,11 @@
     table[:STEPS, :] = jnp.cos(angle)
     table[STEPS:, :] = -jnp.sin(angle)
     window = lax.broadcasted_iota(jnp.int32, (2 * LANES, LANES), 0)
-    window = jnp.where(window < LANES + LANES // 2, window, window - 2 * LANES)
-    row_ids = lax.broadcasted_iota(jnp.int32, (rows_all, LANES), 0)
+    first_tile = jnp.where(window < LANES - HALO, window, window - LANES)
+    second_tile = jnp.where(window < LANES + HALO, window, window - LANES)
+    window = jnp.where(window < LANES, first_tile, second_tile)
+    place = lax.broadcasted_iota(jnp.int32, (rows_all, LANES), 0)
+    row_ids = jnp.where(place < groups, 2 * place, 2 * (place - groups) + 1)
     lanes = lane_ids((rows_all, LANES))
     row_lanes = lane_ids((1, LANES))
 
@@ -242,24 +245,38 @@
 def step_fields(groups, center, halos, shades, inject, snaps, finals):
     rows_all = 2 * groups
     lanes = lane_ids((rows_all, LANES))
-    row_ids = lax.broadcasted_iota(jnp.int32, (rows_all, 2 * LANES), 0)
+    place = lax.broadcasted_iota(jnp.int32, (groups, LANES), 0)
 
     def extended(at, role, slot):
         middle = center[at * rows_all : (at + 1) * rows_all, :]
         halo = halos[role * rows_all : (role + 1) * rows_all, :]
         after = pltpu.roll(halo, (LANES + LANES // 2 - HALO * slot) % LANES, 1)
         before = pltpu.roll(halo, (2 * LANES - HALO - HALO * slot) % LANES, 1)
-        side = jnp.where(lanes < HALO, after, jnp.where(lanes >= LANES - HALO, before, 0.0))
-        return jnp.concatenate([middle, side], axis=1)
+        first = jnp.where(lanes >= LANES - HALO, before, middle)
+        second = jnp.where(lanes < HALO, after, middle)
+        return jnp.concatenate([first, second], axis=0)
+
+    def own(value):
+        return jnp.where(lanes < LANES // 2, value[:rows_all, :], value[rows_all:, :])
 
     def up(value):
-        return jnp.where(row_ids < rows_all - 1, pltpu.roll(value, rows_all - 1, 0), 0.0)
+        parts = []
+        for at in (0, rows_all):
+            shifted = pltpu.roll(value[at : at + groups, :], groups - 1, 0)
+            shifted = jnp.where(place < groups - 1, shifted, 0.0)
+            parts += [value[at + groups : at + rows_all, :], shifted]
+        return jnp.concatenate(parts, axis=0)
 
     def down(value):
-        return jnp.where(row_ids > 0, pltpu.roll(value, 1, 0), 0.0)
+        parts = []
+        for at in (0, rows_all):
+            shifted = pltpu.roll(value[at + groups : at + rows_all, :], 1, 0)
+            shifted = jnp.where(place > 0, shifted, 0.0)
+            parts += [shifted, value[at : at + groups, :]]
+        return jnp.concatenate(parts, axis=0)
 
     def after(value):
-        return pltpu.roll(value, 2 * LANES - 1, 1)
+        return pltpu.roll(value, LANES - 1, 1)
 
     def before(value):
         return pltpu.roll(value, 1, 1)
@@ -271,30 +288,40 @@
         for kind in range(NMAT):
             row = prop * NMAT + kind
             shade = shades[row : row + 1, :]
-            shade = jnp.broadcast_to(jnp.concatenate([shade, shade], axis=1), which.shape)
+            shade = jnp.broadcast_to(shade, which.shape)
             value = jnp.where(which == kind + 1.0, shade, value)
         props.append(value)
     buoyancy, lame_first, lame_second = props
     stiff = lame_first + 2.0 * lame_second
-    for role in range(2):
-        vel_x, vel_z, sig_xx, sig_zz, sig_xz = (
-            extended(role * NFIELD + field, role, field) for field in range(NFIELD)
-        )
-        for tick in range(STEPS):
+    states = [
+        tuple(extended(role * NFIELD + field, role, field) for field in range(NFIELD))
+        for role in range(2)
+    ]
+    for tick in range(STEPS):
+        for role in range(2):
+            vel_x, vel_z, sig_xx, sig_zz, sig_xz = states[role]
             vel_x = vel_x + buoyancy * ((up(sig_xx) - sig_xx) + (sig_xz - before(sig_xz)))
             vel_z = vel_z + buoyancy * ((sig_xz - down(sig_xz)) + (after(sig_zz) - sig_zz))
+            for part, value in enumerate((vel_x, vel_z)):
+                at = ((role * STEPS + tick) * 2 + part) * rows_all
+                rounded = own(value).astype(jnp.bfloat16).astype(jnp.float32)
+                for k in range(2):
+                    half = rounded[k * groups : (k + 1) * groups, :]
+                    snaps[pl.ds(at + k, groups, stride=2), :] = half
+            states[role] = (vel_x, vel_z, sig_xx, sig_zz, sig_xz)
+        for role in range(2):
+            vel_x, vel_z, sig_xx, sig_zz, sig_xz = states[role]
             source = inject[role, tick * rows_all : (tick + 1) * rows_all, :]
+            source = jnp.concatenate([source[:, :LANES], source[:, LANES:]], axis=0)
             strain_x = vel_x - down(vel_x)
             strain_z = vel_z - before(vel_z)
             sig_xx = sig_xx + (stiff * strain_x + lame_first * strain_z) + source
             sig_zz = sig_zz + (lame_first * strain_x + stiff * strain_z) + source
             sig_xz = sig_xz + lame_second * ((after(vel_x) - vel_x) + (up(vel_z) - vel_z))
-            for part, value in enumerate((vel_x, vel_z)):
-                at = ((role * STEPS + tick) * 2 + part) * rows_all
-                rounded = value[:, :LANES].astype(jnp.bfloat16).astype(jnp.float32)
-                snaps[at : at + rows_all, :] = rounded
-        for field, value in enumerate((vel_x, vel_z, sig_xx, sig_zz, sig_xz)):
-            finals[role, field] = value[:, :LANES]
+            states[role] = (vel_x, vel_z, sig_xx, sig_zz, sig_xz)
+    for role in range(2):
+        for field in range(NFIELD):
+            finals[role, field] = own(states[role][field])
 
 
 def correlate(groups, freqs, received, row_snaps, table, weights, gradient):
@@ -371,7 +398,10 @@
     prepare(groups, count, decoded, inject, table, weights)
     step_fields(groups, center, halos, shades, inject, snaps, finals)
     for field in range(NFIELD):
-        own_fields[field] = finals[own_role, field, pl.ds(2 * own_group, 2), :]
+        for k in range(2):
+            own_fields[field, k : k + 1, :] = finals[
+                own_role, field, pl.ds(own_group + k * groups, 1), :
+            ]
     copies = [pltpu.make_async_copy(own_fields, fields_out, sems.at[0])]
     copies[0].start()
     base = own_role * (STEPS * 2 * rows_all)

time: 38.2 us -> 38.1 us (level)
  no operation moved by 1% of the time
where the time goes in v4:
time: 38.1 us; the launch traced here: 37.9 us
  starting transfers between devices  21.5 us (56%)
  waiting for transfers between devices  10.6 us (28%)
  Pallas kernels  5.11 us (13%)
  between operations  0.69 us (2%)
    ppermute x1, starting transfers between devices, program(): from_chip = lax.ppermute(edge_chip, 'space', swaps(size, 0))  16 us
    all_to_all x1, waiting for transfers between devices, program(): received = lax.all_to_all(message, ('role', 'freq'), 0, 0, tiled=True)  7.92 us
    all_to_all x1, starting transfers between devices, program(): received = lax.all_to_all(message, ('role', 'freq'), 0, 0, tiled=True)  3.55 us
    ppermute x1, waiting for transfers between devices, program(): from_link = lax.ppermute(edge_link, 'space', swaps(size, 1))  2.65 us
    pallas_call x1, Pallas kernels, program(): pl.pallas_call(functools.partial(finish, groups, freqs, count), out_shape...  2.48 us
    ppermute x1, starting transfers between devices, program(): from_link = lax.ppermute(edge_link, 'space', swaps(size, 1))  1.92 us
    pallas_call x1, Pallas kernels, program(): pl.pallas_call(functools.partial(pack_block, LANES * size), out_shape=[VM...  1.21 us
    pallas_call x1, Pallas kernels, program(): pl.pallas_call(pack_rows, out_shape=VMEM((members, message_rows, LANES),...  0.85 us
  transfers between devices with their start and end apart: 3, of which 2 were waited for; matrix products, arithmetic and copies ran while one was open for 0% of the time, Pallas kernels for 2%

profile of v4, /device:TPU:1, one launch (start us, length us, event | category | flops | bytes accessed | tf_op | source)
XLA Modules:
  0.0 37.9 jit_solution(6486085536081380657)
XLA Ops:
  0.6 1.2 %pack_block.1 = (f32[16,128]{1,0:T(8,128)S(1)}, f32[2,128]{1,0:T(2,128)S(1)}, f32[2,128]{1,0:T(2,128)S(1)}, f32[1024,128]{1,0:T(8,128)S(1)}, f32[24,128]{1,0:T(8,128)S(1)}) custom-call(f32[5,2,128]{2,1,0:T(2,128)} %bitcast.8, s32[2,128]{1,0:T(2,128)} %ids_in.1, f32[3,8]{1,0:T(4,128)} %material_in.1, s32[1,16]{1,0:T(1,128)} %cells_in.1, s32[1,16]{1,0:T(1,128)} %bitcast.10, ...), custom_call_target="tpu_custom_call" | custom-call | flops 100000 | bytes 40000 | tf_op jit(solution)/shard_map/pack_block/pallas_call | solution.py:480
  1.9 16.0 %collective-permute-start = (f32[2,128]{1,0:T(2,128)S(1)}, f32[2,128]{1,0:T(2,128)S(1)}, u32[]{:S(2)}, u32[]{:S(2)}) collective-permute-start(f32[2,128]{1,0:T(2,128)S(1)} %get-tuple-element.12), channel_id=1, source_target_pairs={{0,8},{16,24},{32,40},{48,56},{64,72},{80,88},{96,104},{112,120},{... | collective-permute-start | bytes 3080 | tf_op jit(solution)/shard_map/ppermute | solution.py:518
  17.9 1.9 %collective-permute-start.1 = (f32[2,128]{1,0:T(2,128)S(1)}, f32[2,128]{1,0:T(2,128)S(1)}, u32[]{:S(2)}, u32[]{:S(2)}) collective-permute-start(f32[2,128]{1,0:T(2,128)S(1)} %get-tuple-element.13), channel_id=1, source_target_pairs={{8,16},{24,32},{40,48},{56,64},{72,80},{88,96},{104,112},{120,128}... | collective-permute-start | bytes 3080 | tf_op jit(solution)/shard_map/ppermute | solution.py:517
  19.8 0.3 pack_spectra.1.row_spectra
  20.1 0.0 collective-permute-done.from_chip
  20.1 2.7 %collective-permute-done.1.from_link = f32[2,128]{1,0:T(2,128)S(1)} collective-permute-done((f32[2,128]{1,0:T(2,128)S(1)}, f32[2,128]{1,0:T(2,128)S(1)}, u32[]{:S(2)}, u32[]{:S(2)}) %collective-permute-start.1) | collective-permute-done | bytes 1056 | tf_op jit(solution)/shard_map/ppermute | solution.py:517
  22.8 0.8 %pack_rows.1 = bf16[16,96,128]{2,1,0:T(8,128)(2,1)} custom-call(f32[16,128]{1,0:T(8,128)S(1)} %get-tuple-element.11.block, f32[2,128]{1,0:T(2,128)S(1)} %collective-permute-done.from_chip, f32[2,128]{1,0:T(2,128)S(1)} %collective-permute-done.1.from_link, bf16[16,64,128]{2,1,0:T(8,128)(2,1)S(1)} %pack_spectra.1.row_spectra), custom_call_target="tpu_custom_call" | custom-call | flops 100000 | bytes 300000 | tf_op jit(solution)/shard_map/pack_rows/pallas_call | solution.py:539
  23.6 3.6 %all-to-all-start = ((bf16[16,96,128]{2,1,0:T(8,128)(2,1)}), bf16[16,96,128]{2,1,0:T(8,128)(2,1)S(1)}, u32[]{:S(2)}, u32[]{:S(2)}) async-start(bf16[16,96,128]{2,1,0:T(8,128)(2,1)} %pack_rows.1), calls=%async_computation | async-start | bytes 786432 | tf_op jit(solution)/shard_map/all_to_all | solution.py:549
  27.2 0.3 twiddle.1.kron
  27.5 7.9 %all-to-all-done.received = bf16[16,96,128]{2,1,0:T(8,128)(2,1)S(1)} async-done(((bf16[16,96,128]{2,1,0:T(8,128)(2,1)}), bf16[16,96,128]{2,1,0:T(8,128)(2,1)S(1)}, u32[]{:S(2)}, u32[]{:S(2)}) %all-to-all-start) | async-done | bytes 393248 | tf_op jit(solution)/shard_map/all_to_all | solution.py:549
  35.4 2.5 %finish.1 = (f32[5,2,128]{2,1,0:T(2,128)}, f32[1024,128]{1,0:T(8,128)}, f32[1,128]{1,0:T(1,128)}) custom-call(bf16[16,96,128]{2,1,0:T(8,128)(2,1)S(1)} %all-to-all-done.received, bf16[256,64]{1,0:T(8,128)(2,1)S(1)} %twiddle.1.kron, f32[1024,128]{1,0:T(8,128)S(1)} %get-tuple-element.14.spectra, f32[24,128]{1,0:T(8,128)S(1)} %get-tuple-element.15.shades), custom_call_target="tpu_custom_call" | custom-call | flops 20000000 | bytes 2000000 | tf_op jit(solution)/shard_map/finish/pallas_call | solution.py:551
Async XLA Ops:
  1.9 18.3 %collective-permute-start = (f32[2,128]{1,0:T(2,128)S(1)}, f32[2,128]{1,0:T(2,128)S(1)}, u32[]{:S(2)}, u32[]{:S(2)}) collective-permute-start(f32[2,128]{1,0:T(2,128)S(1)} %get-tuple-element.12), channel_id=1, source_target_pairs={{0,8},{16,24},{32,40},{48,56},{64,72},{80,88},{96,104},{112,120},{... | collective-permute-start | bytes 3080 | tf_op jit(solution)/shard_map/ppermute | solution.py:518
  17.9 4.9 %collective-permute-start.1 = (f32[2,128]{1,0:T(2,128)S(1)}, f32[2,128]{1,0:T(2,128)S(1)}, u32[]{:S(2)}, u32[]{:S(2)}) collective-permute-start(f32[2,128]{1,0:T(2,128)S(1)} %get-tuple-element.13), channel_id=1, source_target_pairs={{8,16},{24,32},{40,48},{56,64},{72,80},{88,96},{104,112},{120,128}... | collective-permute-start | bytes 3080 | tf_op jit(solution)/shard_map/ppermute | solution.py:517
  23.6 11.8 %all-to-all-start = ((bf16[16,96,128]{2,1,0:T(8,128)(2,1)}), bf16[16,96,128]{2,1,0:T(8,128)(2,1)S(1)}, u32[]{:S(2)}, u32[]{:S(2)}) async-start(bf16[16,96,128]{2,1,0:T(8,128)(2,1)} %pack_rows.1), calls=%async_computation | async-start | bytes 786432 | tf_op jit(solution)/shard_map/all_to_all | solution.py:549

commit v5 on v4

--- a/solution.py
+++ b/solution.py
@@ -142,7 +142,10 @@
         message[row, 2 * MSG_ROWS :, :] = row_spectra[row]
 
 
-def twiddle(freqs, block, kron):
+def twiddle(freqs, block, kron, waves):
+    lane = lane_ids((STEPS, LANES)).astype(jnp.float32) * (TWO_PI / PERIOD)
+    waves[:STEPS, :] = jnp.cos(lane)
+    waves[STEPS:, :] = -jnp.sin(lane)
     span = 8 * STEPS
     lanes = lax.broadcasted_iota(jnp.int32, (freqs, freqs), 1)
     rows = lax.broadcasted_iota(jnp.int32, (freqs, freqs), 0)
@@ -187,7 +190,7 @@
     gather(center, 2 * NFIELD * rows_all, 0, ROW_IDS)
 
 
-def prepare(groups, count, decoded, inject, table, weights):
+def prepare(groups, count, decoded, waves, inject, table, weights):
     rows_all = 2 * groups
     first_column = lax.axis_index("space") * LANES
 
@@ -202,9 +205,8 @@
     index = joined(AT_INDEX).astype(jnp.int32)
     times = lax.broadcasted_iota(jnp.int32, (STEPS, LANES), 0)
     turns = lax.bitwise_and(index * times, PERIOD - 1)
-    angle = turns.astype(jnp.float32) * (TWO_PI / PERIOD)
-    table[:STEPS, :] = jnp.cos(angle)
-    table[STEPS:, :] = -jnp.sin(angle)
+    table[:STEPS, :] = jnp.take_along_axis(waves[:STEPS, :], turns, axis=1)
+    table[STEPS:, :] = jnp.take_along_axis(waves[STEPS:, :], turns, axis=1)
     window = lax.broadcasted_iota(jnp.int32, (2 * LANES, LANES), 0)
     first_tile = jnp.where(window < LANES - HALO, window, window - LANES)
     second_tile = jnp.where(window < LANES + HALO, window, window - LANES)
@@ -372,6 +374,7 @@
     count,
     received,
     kron,
+    waves,
     spectra,
     shades,
     fields_out,
@@ -395,7 +398,7 @@
     own_role = lax.axis_index("role")
     own_group = lax.axis_index("freq")
     unpack(groups, received, decoded, center, halos)
-    prepare(groups, count, decoded, inject, table, weights)
+    prepare(groups, count, decoded, waves, inject, table, weights)
     step_fields(groups, center, halos, shades, inject, snaps, finals)
     for field in range(NFIELD):
         for k in range(2):
@@ -517,11 +520,14 @@
     from_link = lax.ppermute(edge_link, "space", swaps(size, 1))
     from_chip = lax.ppermute(edge_chip, "space", swaps(size, 0))
 
-    kron = pl.pallas_call(
+    kron, waves = pl.pallas_call(
         functools.partial(twiddle, freqs),
-        out_shape=jax.ShapeDtypeStruct((freqs * 16, STEPS * 8), jnp.bfloat16),
+        out_shape=[
+            jax.ShapeDtypeStruct((freqs * 16, STEPS * 8), jnp.bfloat16),
+            f32(2 * STEPS, LANES),
+        ],
         in_specs=[whole()],
-        out_specs=whole(),
+        out_specs=[whole()] * 2,
         cost_estimate=cost(100_000, 40_000),
         compiler_params=params(512),
         name="twiddle",
@@ -555,7 +561,7 @@
             f32(freqs * PARTS * rows_all, LANES),
             f32(1, LANES),
         ],
-        in_specs=[whole()] * 4,
+        in_specs=[whole()] * 5,
         out_specs=[whole(pl.ANY)] * 3,
         scratch_shapes=[
             VMEM((members * MSG_ROWS, LANES), jnp.float32),
@@ -575,7 +581,7 @@
         cost_estimate=cost(20_000_000, 2_000_000),
         compiler_params=params(4096),
         name="finish",
-    )(received, kron, held, shades)
+    )(received, kron, waves, held, shades)
     return fields_out[None], spectra_out.reshape(spectra.shape), gradient
 
 

time: 38.1 us -> 38.2 us (level)
  no operation moved by 1% of the time
where the time goes in v5:
time: 38.2 us; the launch traced here: 37.9 us
  starting transfers between devices  21.5 us (56%)
  waiting for transfers between devices  10.6 us (28%)
  Pallas kernels  5.13 us (13%)
  between operations  0.69 us (2%)
    ppermute x1, starting transfers between devices, program(): from_chip = lax.ppermute(edge_chip, 'space', swaps(size, 0))  16 us
    all_to_all x1, waiting for transfers between devices, program(): received = lax.all_to_all(message, ('role', 'freq'), 0, 0, tiled=True)  7.92 us
    all_to_all x1, starting transfers between devices, program(): received = lax.all_to_all(message, ('role', 'freq'), 0, 0, tiled=True)  3.55 us
    ppermute x1, waiting for transfers between devices, program(): from_link = lax.ppermute(edge_link, 'space', swaps(size, 1))  2.65 us
    pallas_call x1, Pallas kernels, program(): pl.pallas_call(functools.partial(finish, groups, freqs, count), out_shape...  2.5 us
    ppermute x1, starting transfers between devices, program(): from_link = lax.ppermute(edge_link, 'space', swaps(size, 1))  1.92 us
    pallas_call x1, Pallas kernels, program(): pl.pallas_call(functools.partial(pack_block, LANES * size), out_shape=[VM...  1.21 us
    pallas_call x1, Pallas kernels, program(): pl.pallas_call(pack_rows, out_shape=VMEM((members, message_rows, LANES),...  0.85 us
  transfers between devices with their start and end apart: 3, of which 2 were waited for; matrix products, arithmetic and copies ran while one was open for 0% of the time, Pallas kernels for 2%

profile of v5, /device:TPU:1, one launch (start us, length us, event | category | flops | bytes accessed | tf_op | source)
XLA Modules:
  0.0 37.9 jit_solution(12110737001859263101)
XLA Ops:
  0.6 1.2 %pack_block.1 = (f32[16,128]{1,0:T(8,128)S(1)}, f32[2,128]{1,0:T(2,128)S(1)}, f32[2,128]{1,0:T(2,128)S(1)}, f32[1024,128]{1,0:T(8,128)S(1)}, f32[24,128]{1,0:T(8,128)S(1)}) custom-call(f32[5,2,128]{2,1,0:T(2,128)} %bitcast.8, s32[2,128]{1,0:T(2,128)} %ids_in.1, f32[3,8]{1,0:T(4,128)} %material_in.1, s32[1,16]{1,0:T(1,128)} %cells_in.1, s32[1,16]{1,0:T(1,128)} %bitcast.10, ...), custom_call_target="tpu_custom_call" | custom-call | flops 100000 | bytes 40000 | tf_op jit(solution)/shard_map/pack_block/pallas_call | solution.py:483
  1.9 16.0 %collective-permute-start = (f32[2,128]{1,0:T(2,128)S(1)}, f32[2,128]{1,0:T(2,128)S(1)}, u32[]{:S(2)}, u32[]{:S(2)}) collective-permute-start(f32[2,128]{1,0:T(2,128)S(1)} %get-tuple-element.14), channel_id=1, source_target_pairs={{0,8},{16,24},{32,40},{48,56},{64,72},{80,88},{96,104},{112,120},{... | collective-permute-start | bytes 3080 | tf_op jit(solution)/shard_map/ppermute | solution.py:521
  17.9 1.9 %collective-permute-start.1 = (f32[2,128]{1,0:T(2,128)S(1)}, f32[2,128]{1,0:T(2,128)S(1)}, u32[]{:S(2)}, u32[]{:S(2)}) collective-permute-start(f32[2,128]{1,0:T(2,128)S(1)} %get-tuple-element.15), channel_id=1, source_target_pairs={{8,16},{24,32},{40,48},{56,64},{72,80},{88,96},{104,112},{120,128}... | collective-permute-start | bytes 3080 | tf_op jit(solution)/shard_map/ppermute | solution.py:520
  19.8 0.3 pack_spectra.1.row_spectra
  20.1 0.0 collective-permute-done.from_chip
  20.1 2.7 %collective-permute-done.1.from_link = f32[2,128]{1,0:T(2,128)S(1)} collective-permute-done((f32[2,128]{1,0:T(2,128)S(1)}, f32[2,128]{1,0:T(2,128)S(1)}, u32[]{:S(2)}, u32[]{:S(2)}) %collective-permute-start.1) | collective-permute-done | bytes 1056 | tf_op jit(solution)/shard_map/ppermute | solution.py:520
  22.8 0.8 %pack_rows.1 = bf16[16,96,128]{2,1,0:T(8,128)(2,1)} custom-call(f32[16,128]{1,0:T(8,128)S(1)} %get-tuple-element.13.block, f32[2,128]{1,0:T(2,128)S(1)} %collective-permute-done.from_chip, f32[2,128]{1,0:T(2,128)S(1)} %collective-permute-done.1.from_link, bf16[16,64,128]{2,1,0:T(8,128)(2,1)S(1)} %pack_spectra.1.row_spectra), custom_call_target="tpu_custom_call" | custom-call | flops 100000 | bytes 300000 | tf_op jit(solution)/shard_map/pack_rows/pallas_call | solution.py:545
  23.6 3.6 %all-to-all-start = ((bf16[16,96,128]{2,1,0:T(8,128)(2,1)}), bf16[16,96,128]{2,1,0:T(8,128)(2,1)S(1)}, u32[]{:S(2)}, u32[]{:S(2)}) async-start(bf16[16,96,128]{2,1,0:T(8,128)(2,1)} %pack_rows.1), calls=%async_computation | async-start | bytes 786432 | tf_op jit(solution)/shard_map/all_to_all | solution.py:555
  27.2 0.3 twiddle.1
  27.5 7.9 %all-to-all-done.received = bf16[16,96,128]{2,1,0:T(8,128)(2,1)S(1)} async-done(((bf16[16,96,128]{2,1,0:T(8,128)(2,1)}), bf16[16,96,128]{2,1,0:T(8,128)(2,1)S(1)}, u32[]{:S(2)}, u32[]{:S(2)}) %all-to-all-start) | async-done | bytes 393248 | tf_op jit(solution)/shard_map/all_to_all | solution.py:555
  35.4 2.5 %finish.1 = (f32[5,2,128]{2,1,0:T(2,128)}, f32[1024,128]{1,0:T(8,128)}, f32[1,128]{1,0:T(1,128)}) custom-call(bf16[16,96,128]{2,1,0:T(8,128)(2,1)S(1)} %all-to-all-done.received, bf16[256,64]{1,0:T(8,128)(2,1)S(1)} %get-tuple-element.17.kron, f32[16,128]{1,0:T(8,128)S(1)} %get-tuple-element.18.waves, f32[1024,128]{1,0:T(8,128)S(1)} %get-tuple-element.16.spectra, ...), custom_call_target="tpu_custom_call" | custom-call | flops 20000000 | bytes 2000000 | tf_op jit(solution)/shard_map/finish/pallas_call | solution.py:557
Async XLA Ops:
  1.9 18.3 %collective-permute-start = (f32[2,128]{1,0:T(2,128)S(1)}, f32[2,128]{1,0:T(2,128)S(1)}, u32[]{:S(2)}, u32[]{:S(2)}) collective-permute-start(f32[2,128]{1,0:T(2,128)S(1)} %get-tuple-element.14), channel_id=1, source_target_pairs={{0,8},{16,24},{32,40},{48,56},{64,72},{80,88},{96,104},{112,120},{... | collective-permute-start | bytes 3080 | tf_op jit(solution)/shard_map/ppermute | solution.py:521
  17.9 4.9 %collective-permute-start.1 = (f32[2,128]{1,0:T(2,128)S(1)}, f32[2,128]{1,0:T(2,128)S(1)}, u32[]{:S(2)}, u32[]{:S(2)}) collective-permute-start(f32[2,128]{1,0:T(2,128)S(1)} %get-tuple-element.15), channel_id=1, source_target_pairs={{8,16},{24,32},{40,48},{56,64},{72,80},{88,96},{104,112},{120,128}... | collective-permute-start | bytes 3080 | tf_op jit(solution)/shard_map/ppermute | solution.py:520
  23.6 11.8 %all-to-all-start = ((bf16[16,96,128]{2,1,0:T(8,128)(2,1)}), bf16[16,96,128]{2,1,0:T(8,128)(2,1)S(1)}, u32[]{:S(2)}, u32[]{:S(2)}) async-start(bf16[16,96,128]{2,1,0:T(8,128)(2,1)} %pack_rows.1), calls=%async_computation | async-start | bytes 786432 | tf_op jit(solution)/shard_map/all_to_all | solution.py:555
